TPU v7x, 32 devices: a 4x4x1 block of a 4x4x8 slice. The times are simulated.
32 devices in a mesh: pairs: 1 (over z), cols: 4 (over y), rows: 8 (over x, core).
Axes of the slice: x: 4, y: 4, z: 1, core: 2. Of those that a mesh axis runs over, the one named last changes fastest.
The devices are a block of a 4x4x8 slice.
Arguments:
- C1: float32 [8192, 8192], P(('pairs', 'rows'), 'cols')
- C2: float32 [1024, 1024], P(('pairs', 'rows'), 'cols')
- T0: float32 [8192, 1024], P(('pairs', 'rows'), 'cols')
- p: float32 [8192], P(('pairs', 'rows'))
- q: float32 [1024], P(('pairs', 'cols'))
- eps: float32 [8], P('pairs')
Outputs:
- output 1: float32 [8192, 1024], P(('pairs', 'rows'), 'cols')
- output 2: float32 [1], P('pairs')
All inputs are finite; a program needn't handle non-finite values.
Results may differ from a plain program's by a relative error of at most 0.001.
Values are sent between devices in bfloat16 or wider.
A program may use at most 768 MiB of HBM per device.

v0:
```python
import jax
import jax.numpy as jnp
from jax import lax
from jax.sharding import PartitionSpec as P

SWEEPS = 10


def solution(mesh):
    grid_spec = P(("pairs", "rows"), "cols")

    def local_fn(c1_blk, c2_blk, t0_blk, p_blk, q_blk, eps_blk):
        col_pos = lax.axis_index("cols")
        row_pos = lax.axis_index("rows")
        c1_width = c1_blk.shape[1]
        c2_height = c2_blk.shape[0]
        p_full = lax.all_gather(p_blk, "rows", tiled=True)
        q_full = lax.all_gather(q_blk, "cols", tiled=True)
        p_piece = lax.dynamic_slice_in_dim(p_full, col_pos * c1_width, c1_width)
        q_piece = lax.dynamic_slice_in_dim(q_full, row_pos * c2_height, c2_height)
        row_term = lax.psum(jnp.sum(c1_blk * c1_blk * p_piece[None, :], axis=1), "cols")
        col_term = lax.psum(jnp.sum(c2_blk * c2_blk * q_piece[:, None], axis=0), "rows")
        const_blk = row_term[:, None] + col_term[None, :]
        c1_panel = lax.all_gather(c1_blk.astype(jnp.bfloat16), "cols", axis=1, tiled=True)
        c2_panel = lax.all_gather(c2_blk.astype(jnp.bfloat16), "rows", axis=0, tiled=True)

        def cost_of(plan_blk):
            plan_panel = lax.all_gather(plan_blk.astype(jnp.bfloat16), "rows", axis=0, tiled=True)
            lead_blk = jnp.dot(c1_panel, plan_panel, preferred_element_type=jnp.float32)
            lead_panel = lax.all_gather(lead_blk.astype(jnp.bfloat16), "cols", axis=1, tiled=True)
            cross_blk = jnp.dot(lead_panel, c2_panel, preferred_element_type=jnp.float32)
            return const_blk - 2.0 * cross_blk

        def balance(kernel):
            def sweep(sweep_idx, scales):
                row_scale = p_blk / lax.psum(jnp.sum(kernel * scales[1][None, :], axis=1), "cols")
                col_scale = q_blk / lax.psum(jnp.sum(kernel * row_scale[:, None], axis=0), "rows")
                return row_scale, col_scale
            row_scale, col_scale = lax.fori_loop(0, SWEEPS, sweep, (jnp.ones_like(p_blk), jnp.ones_like(q_blk)))
            return row_scale[:, None] * kernel * col_scale[None, :]

        plan_blk = t0_blk
        for step_idx in range(eps_blk.shape[0]):
            cost_blk = cost_of(plan_blk)
            row_shift = lax.pmin(jnp.min(cost_blk, axis=1), "cols")
            kernel = jnp.exp(-(cost_blk - row_shift[:, None]) / eps_blk[step_idx])
            plan_blk = balance(kernel)
        cost_blk = cost_of(plan_blk)
        loss_val = lax.psum(jnp.sum(cost_blk * plan_blk), ("rows", "cols"))
        return plan_blk, loss_val.reshape(1)

    return jax.shard_map(local_fn, mesh=mesh, in_specs=(grid_spec, grid_spec, grid_spec, P(("pairs", "rows")), P(("pairs", "cols")), P("pairs")), out_specs=(grid_spec, P("pairs")), check_vma=False)
```

profile of v0, /device:TPU:97, one launch (start us, length us, event | category | flops | bytes accessed | tf_op | source)
XLA Modules:
  0.0 2717.5 jit_solution(5890094502860463620)
XLA Ops:
  9.5 19.9 all_gather.66
  44.1 153.2 %all-gather.21.cloned.1.call-done = bf16[1024,8192]{1,0:T(8,128)(2,1)} async-done(((bf16[1024,2048]{1,0:T(8,128)(2,1)}), bf16[1024,8192]{1,0:T(8,128)(2,1)}) %all-gather.21.cloned.1.call-update) | async-done | bytes 16777232 | tf_op jit(solution)/shard_map/all_gather | solution.py:24
  216.6 15.1 psum.134
  239.4 17.8 all_gather.71
  268.7 225.2 %while.104 = (s32[]{:T(128)}, f32[1024]{0:T(1024)}, f32[256]{0:T(256)S(1)}, f32[1024,256]{1,0:T(8,128)S(1)}, f32[1024]{0:T(1024)S(1)}, /*index=5*/f32[256]{0:T(256)S(1)}, s32[]{:T(128)}, s32[]{:T(128)}) while((s32[]{:T(128)}, f32[1024]{0:T(1024)}, f32[256]{0:T(256)S(1)}, f32[1024,256]{1,0:T(8,128)S(1)}, f32[1024]{0:T(1024)S(1)}, ...), condition=%wide.region_11.0_spmd.clone, body=%wide.region_6.0_spmd.clone.sunk | while | flops 1050115 | bytes 2151547 | solution.py:39
  275.6 21.9 psum.169
  305.1 14.5 psum.169
  326.6 14.5 psum.169
  348.7 14.5 psum.169
  370.2 14.5 psum.169
  392.2 14.5 psum.169
  413.7 14.5 psum.169
  457.3 14.5 psum.169
  496.6 26.2 all-gather.27.cloned.1.call-done
  535.3 27.4 %all-gather.29.cloned.1.call-done = bf16[1024,1024]{0,1:T(8,128)(2,1)} async-done(((bf16[1024,256]{0,1:T(8,128)(2,1)}), bf16[1024,1024]{0,1:T(8,128)(2,1)}) %all-gather.29.cloned.1.call-update) | async-done | bytes 2097168 | tf_op jit(solution)/shard_map/all_gather | solution.py:30
  573.6 220.0 %while.105 = (s32[]{:T(128)}, f32[1024]{0:T(1024)}, f32[256]{0:T(256)S(1)}, f32[1024,256]{1,0:T(8,128)S(1)}, f32[1024]{0:T(1024)S(1)}, /*index=5*/f32[256]{0:T(256)S(1)}, s32[]{:T(128)}, s32[]{:T(128)}) while((s32[]{:T(128)}, f32[1024]{0:T(1024)}, f32[256]{0:T(256)S(1)}, f32[1024,256]{1,0:T(8,128)S(1)}, f32[1024]{0:T(1024)S(1)}, ...), condition=%wide.region_19.0_spmd.clone, body=%wide.region_14.0_spmd.clone.sunk | while | flops 1050115 | bytes 2151547 | solution.py:39
  580.9 16.8 psum.171
  626.7 14.5 psum.171
  691.9 14.5 psum.171
  757.4 14.5 psum.171
  796.0 26.7 all-gather.31.cloned.1.call-done
  835.5 27.2 %all-gather.33.cloned.1.call-done = bf16[1024,1024]{0,1:T(8,128)(2,1)} async-done(((bf16[1024,256]{0,1:T(8,128)(2,1)}), bf16[1024,1024]{0,1:T(8,128)(2,1)}) %all-gather.33.cloned.1.call-update) | async-done | bytes 2097168 | tf_op jit(solution)/shard_map/all_gather | solution.py:30
  873.6 220.0 %while.106 = (s32[]{:T(128)}, f32[1024]{0:T(1024)}, f32[256]{0:T(256)S(1)}, f32[1024,256]{1,0:T(8,128)S(1)}, f32[1024]{0:T(1024)S(1)}, /*index=5*/f32[256]{0:T(256)S(1)}, s32[]{:T(128)}, s32[]{:T(128)}) while((s32[]{:T(128)}, f32[1024]{0:T(1024)}, f32[256]{0:T(256)S(1)}, f32[1024,256]{1,0:T(8,128)S(1)}, f32[1024]{0:T(1024)S(1)}, ...), condition=%wide.region_27.0_spmd.clone, body=%wide.region_22.0_spmd.clone.sunk | while | flops 1050115 | bytes 2151547 | solution.py:39
  880.9 16.8 psum.173
  948.3 14.5 psum.173
  1013.9 14.5 psum.173
  1079.0 14.5 psum.173
  1096.0 26.7 all-gather.35.cloned.1.call-done
  1135.3 27.4 %all-gather.37.cloned.1.call-done = bf16[1024,1024]{0,1:T(8,128)(2,1)} async-done(((bf16[1024,256]{0,1:T(8,128)(2,1)}), bf16[1024,1024]{0,1:T(8,128)(2,1)}) %all-gather.37.cloned.1.call-update) | async-done | bytes 2097168 | tf_op jit(solution)/shard_map/all_gather | solution.py:30
  1173.6 220.0 %while.107 = (s32[]{:T(128)}, f32[1024]{0:T(1024)}, f32[256]{0:T(256)S(1)}, f32[1024,256]{1,0:T(8,128)S(1)}, f32[1024]{0:T(1024)S(1)}, /*index=5*/f32[256]{0:T(256)S(1)}, s32[]{:T(128)}, s32[]{:T(128)}) while((s32[]{:T(128)}, f32[1024]{0:T(1024)}, f32[256]{0:T(256)S(1)}, f32[1024,256]{1,0:T(8,128)S(1)}, f32[1024]{0:T(1024)S(1)}, ...), condition=%wide.region_35.0_spmd.clone, body=%wide.region_30.0_spmd.clone.sunk | while | flops 1050115 | bytes 2151547 | solution.py:39
  1180.9 16.8 psum.175
  1291.9 14.5 psum.175
  1313.9 14.5 psum.175
  1396.5 26.3 all-gather.39.cloned.1.call-done
  1435.3 27.4 %all-gather.41.cloned.1.call-done = bf16[1024,1024]{0,1:T(8,128)(2,1)} async-done(((bf16[1024,256]{0,1:T(8,128)(2,1)}), bf16[1024,1024]{0,1:T(8,128)(2,1)}) %all-gather.41.cloned.1.call-update) | async-done | bytes 2097168 | tf_op jit(solution)/shard_map/all_gather | solution.py:30
  1473.6 220.0 %while.108 = (s32[]{:T(128)}, f32[1024]{0:T(1024)}, f32[256]{0:T(256)S(1)}, f32[1024,256]{1,0:T(8,128)S(1)}, f32[1024]{0:T(1024)S(1)}, /*index=5*/f32[256]{0:T(256)S(1)}, s32[]{:T(128)}, s32[]{:T(128)}) while((s32[]{:T(128)}, f32[1024]{0:T(1024)}, f32[256]{0:T(256)S(1)}, f32[1024,256]{1,0:T(8,128)S(1)}, f32[1024]{0:T(1024)S(1)}, ...), condition=%wide.region_43.0_spmd.clone, body=%wide.region_38.0_spmd.clone.sunk | while | flops 1050115 | bytes 2151547 | solution.py:39
  1480.9 16.8 psum.177
  1548.3 14.5 psum.177
  1613.9 14.5 psum.177
  1679.1 14.5 psum.177
  1696.1 26.7 all-gather.43.cloned.1.call-done
  1735.6 27.2 %all-gather.45.cloned.1.call-done = bf16[1024,1024]{0,1:T(8,128)(2,1)} async-done(((bf16[1024,256]{0,1:T(8,128)(2,1)}), bf16[1024,1024]{0,1:T(8,128)(2,1)}) %all-gather.45.cloned.1.call-update) | async-done | bytes 2097168 | tf_op jit(solution)/shard_map/all_gather | solution.py:30
  1773.6 220.0 %while.109 = (s32[]{:T(128)}, f32[1024]{0:T(1024)}, f32[256]{0:T(256)S(1)}, f32[1024,256]{1,0:T(8,128)S(1)}, f32[1024]{0:T(1024)S(1)}, /*index=5*/f32[256]{0:T(256)S(1)}, s32[]{:T(128)}, s32[]{:T(128)}) while((s32[]{:T(128)}, f32[1024]{0:T(1024)}, f32[256]{0:T(256)S(1)}, f32[1024,256]{1,0:T(8,128)S(1)}, f32[1024]{0:T(1024)S(1)}, ...), condition=%wide.region_51.0_spmd.clone, body=%wide.region_46.0_spmd.clone.sunk | while | flops 1050115 | bytes 2151547 | solution.py:39
  1780.9 16.8 psum.179
  1804.8 14.5 psum.179
  1870.3 14.5 psum.179
  1935.5 14.5 psum.179
  1996.0 26.7 all-gather.47.cloned.1.call-done
  2035.2 27.4 %all-gather.49.cloned.1.call-done = bf16[1024,1024]{0,1:T(8,128)(2,1)} async-done(((bf16[1024,256]{0,1:T(8,128)(2,1)}), bf16[1024,1024]{0,1:T(8,128)(2,1)}) %all-gather.49.cloned.1.call-update) | async-done | bytes 2097168 | tf_op jit(solution)/shard_map/all_gather | solution.py:30
  2073.5 220.0 %while.110 = (s32[]{:T(128)}, f32[1024]{0:T(1024)}, f32[256]{0:T(256)S(1)}, f32[1024,256]{1,0:T(8,128)S(1)}, f32[1024]{0:T(1024)S(1)}, /*index=5*/f32[256]{0:T(256)S(1)}, s32[]{:T(128)}, s32[]{:T(128)}) while((s32[]{:T(128)}, f32[1024]{0:T(1024)}, f32[256]{0:T(256)S(1)}, f32[1024,256]{1,0:T(8,128)S(1)}, f32[1024]{0:T(1024)S(1)}, ...), condition=%wide.region_59.0_spmd.clone, body=%wide.region_54.0_spmd.clone.sunk | while | flops 1050115 | bytes 2151547 | solution.py:39
  2080.8 16.8 psum.181
  2191.8 14.5 psum.181
  2213.8 14.5 psum.181
  2296.1 26.5 all-gather.51.cloned.1.call-done
  2335.1 27.4 %all-gather.53.cloned.1.call-done = bf16[1024,1024]{0,1:T(8,128)(2,1)} async-done(((bf16[1024,256]{0,1:T(8,128)(2,1)}), bf16[1024,1024]{0,1:T(8,128)(2,1)}) %all-gather.53.cloned.1.call-update) | async-done | bytes 2097168 | tf_op jit(solution)/shard_map/all_gather | solution.py:30
  2373.4 220.0 %while.111 = (s32[]{:T(128)}, f32[1024]{0:T(1024)}, f32[256]{0:T(256)S(1)}, f32[1024,256]{1,0:T(8,128)S(1)}, f32[1024]{0:T(1024)S(1)}, /*index=5*/f32[256]{0:T(256)S(1)}, s32[]{:T(128)}, s32[]{:T(128)}) while((s32[]{:T(128)}, f32[1024]{0:T(1024)}, f32[256]{0:T(256)S(1)}, f32[1024,256]{1,0:T(8,128)S(1)}, f32[1024]{0:T(1024)S(1)}, ...), condition=%wide.region_67.0_spmd.clone, body=%wide.region_62.0_spmd.clone.sunk | while | flops 1050115 | bytes 2151547 | solution.py:39
  2380.7 16.8 psum.183
  2404.6 14.5 psum.183
  2426.5 14.5 psum.183
  2535.3 14.5 psum.183
  2557.3 14.5 psum.183
  2596.1 26.5 all-gather.55.cloned.1.call-done
  2636.4 26.2 all-gather.57.cloned.1.call-done
  2665.7 45.1 %psum.135 = f32[1]{0:T(128)} all-reduce(f32[1]{0:T(128)} %bitcast.18), channel_id=1, replica_groups=mesh['pairs'=1,'cols'=4,'rows'=8] {'rows','cols'}, use_global_device_ids=true, to_apply=%region_69.0 | all-reduce | flops 1 | bytes 8 | tf_op jit(solution)/shard_map/psum | solution.py:49
  (826 shorter events, 1488.1 us)
Async XLA Ops:
  7.2 36.9 %all-gather.23.cloned.1.call-start = ((), (), s32[]{:S(2)}) async-start(), calls=%async_computation.1 | async-start | bytes 4718592 | tf_op jit(solution)/shard_map/all_gather | solution.py:28
  9.4 188.0 %all-gather.21.cloned.1.call-start = ((), (), s32[]{:S(2)}) async-start(), calls=%async_computation | async-start | bytes 20971520 | tf_op jit(solution)/shard_map/all_gather | solution.py:24
  38.6 171.1 %copy-start.1 = (f32[256]{0:T(256)S(1)}, f32[256]{0:T(256)}, u32[]{:S(2)}) copy-start(f32[256]{0:T(256)} %param.26) | copy-start | bytes 3076
  38.6 177.8 %copy-start.19 = (f32[128,256]{1,0:T(8,128)S(1)}, f32[128,256]{1,0:T(8,128)}, u32[]{:S(2)}) copy-start(f32[128,256]{1,0:T(8,128)} %param.23) | copy-start | bytes 393220
  38.7 200.1 %copy-start.20 = (f32[8]{0:T(128)S(1)}, f32[8]{0:T(128)}, u32[]{:S(2)}) copy-start(f32[8]{0:T(128)} %param.27) | copy-start | bytes 100
  38.7 218.6 %all-gather.25.cloned.1.call-start = ((), (), s32[]{:S(2)}) async-start(), calls=%async_computation.2 | async-start | bytes 2621440 | tf_op jit(solution)/shard_map/all_gather | solution.py:30
  209.6 313.1 %all-gather.27.cloned.1.call-start = ((), (), s32[]{:S(2)}) async-start(), calls=%async_computation.3 | async-start | bytes 4718592 | tf_op jit(solution)/shard_map/all_gather | solution.py:28
  275.4 22.1 copy-start.12
  304.9 14.8 copy-start.12
  326.4 14.8 copy-start.12
  348.4 14.8 copy-start.12
  369.9 14.8 copy-start.12
  392.0 14.8 copy-start.12
  413.5 14.8 copy-start.12
  435.6 14.8 copy-start.12
  457.1 14.8 copy-start.12
  479.2 14.8 copy-start.12
  496.3 66.4 %copy-start.3 = (bf16[1024,256]{1,0:T(8,128)(2,1)S(1)}, bf16[1024,256]{1,0:T(8,128)(2,1)}, u32[]{:S(2)}) copy-start(bf16[1024,256]{1,0:T(8,128)(2,1)} %copy-done.2) | copy-start | bytes 1572868
  496.3 66.3 %all-gather.29.cloned.1.call-start = ((), (), s32[]{:S(2)}) async-start(), calls=%async_computation.4 | async-start | bytes 2621440 | tf_op jit(solution)/shard_map/all_gather | solution.py:30
  535.2 287.6 %all-gather.31.cloned.1.call-start = ((), (), s32[]{:S(2)}) async-start(), calls=%async_computation.5 | async-start | bytes 4718592 | tf_op jit(solution)/shard_map/all_gather | solution.py:28
  580.6 17.0 copy-start.13
  626.5 14.8 copy-start.13
  648.1 14.8 copy-start.13
  670.1 14.8 copy-start.13
  691.6 14.8 copy-start.13
  713.6 14.8 copy-start.13
  735.2 14.8 copy-start.13
  757.2 14.8 copy-start.13
  778.8 14.8 copy-start.13
  796.0 66.7 %copy-start.4 = (bf16[1024,256]{1,0:T(8,128)(2,1)S(1)}, bf16[1024,256]{1,0:T(8,128)(2,1)}, u32[]{:S(2)}) copy-start(bf16[1024,256]{1,0:T(8,128)(2,1)} %copy-done.2) | copy-start | bytes 1572868
  796.0 66.7 %all-gather.33.cloned.1.call-start = ((), (), s32[]{:S(2)}) async-start(), calls=%async_computation.6 | async-start | bytes 2621440 | tf_op jit(solution)/shard_map/all_gather | solution.py:30
  835.2 287.6 %all-gather.35.cloned.1.call-start = ((), (), s32[]{:S(2)}) async-start(), calls=%async_computation.7 | async-start | bytes 4718592 | tf_op jit(solution)/shard_map/all_gather | solution.py:28
  880.6 17.0 copy-start.14
  904.5 14.8 copy-start.14
  948.1 14.8 copy-start.14
  970.1 14.8 copy-start.14
  991.6 14.8 copy-start.14
  1013.6 14.8 copy-start.14
  1035.2 14.8 copy-start.14
  1078.8 14.8 copy-start.14
  1096.0 66.7 %copy-start.5 = (bf16[1024,256]{1,0:T(8,128)(2,1)S(1)}, bf16[1024,256]{1,0:T(8,128)(2,1)}, u32[]{:S(2)}) copy-start(bf16[1024,256]{1,0:T(8,128)(2,1)} %copy-done.2) | copy-start | bytes 1572868
  1096.0 66.7 %all-gather.37.cloned.1.call-start = ((), (), s32[]{:S(2)}) async-start(), calls=%async_computation.8 | async-start | bytes 2621440 | tf_op jit(solution)/shard_map/all_gather | solution.py:30
  1135.2 287.6 %all-gather.39.cloned.1.call-start = ((), (), s32[]{:S(2)}) async-start(), calls=%async_computation.9 | async-start | bytes 4718592 | tf_op jit(solution)/shard_map/all_gather | solution.py:28
  1180.7 17.0 copy-start.15
  1204.5 14.8 copy-start.15
  1226.5 14.8 copy-start.15
  1396.0 66.7 %copy-start.6 = (bf16[1024,256]{1,0:T(8,128)(2,1)S(1)}, bf16[1024,256]{1,0:T(8,128)(2,1)}, u32[]{:S(2)}) copy-start(bf16[1024,256]{1,0:T(8,128)(2,1)} %copy-done.2) | copy-start | bytes 1572868
  1396.0 66.7 %all-gather.41.cloned.1.call-start = ((), (), s32[]{:S(2)}) async-start(), calls=%async_computation.10 | async-start | bytes 2621440 | tf_op jit(solution)/shard_map/all_gather | solution.py:30
  1435.2 287.7 %all-gather.43.cloned.1.call-start = ((), (), s32[]{:S(2)}) async-start(), calls=%async_computation.11 | async-start | bytes 4718592 | tf_op jit(solution)/shard_map/all_gather | solution.py:28
  1480.7 17.0 copy-start.16
  1696.1 66.7 %copy-start.7 = (bf16[1024,256]{1,0:T(8,128)(2,1)S(1)}, bf16[1024,256]{1,0:T(8,128)(2,1)}, u32[]{:S(2)}) copy-start(bf16[1024,256]{1,0:T(8,128)(2,1)} %copy-done.2) | copy-start | bytes 1572868
  1696.1 66.7 %all-gather.45.cloned.1.call-start = ((), (), s32[]{:S(2)}) async-start(), calls=%async_computation.12 | async-start | bytes 2621440 | tf_op jit(solution)/shard_map/all_gather | solution.py:30
  1735.3 287.4 %all-gather.47.cloned.1.call-start = ((), (), s32[]{:S(2)}) async-start(), calls=%async_computation.13 | async-start | bytes 4718592 | tf_op jit(solution)/shard_map/all_gather | solution.py:28
  1780.7 17.0 copy-start.17
  1995.9 66.7 %copy-start.8 = (bf16[1024,256]{1,0:T(8,128)(2,1)S(1)}, bf16[1024,256]{1,0:T(8,128)(2,1)}, u32[]{:S(2)}) copy-start(bf16[1024,256]{1,0:T(8,128)(2,1)} %copy-done.2) | copy-start | bytes 1572868
  1995.9 66.7 %all-gather.49.cloned.1.call-start = ((), (), s32[]{:S(2)}) async-start(), calls=%async_computation.14 | async-start | bytes 2621440 | tf_op jit(solution)/shard_map/all_gather | solution.py:30
  2035.2 287.4 %all-gather.51.cloned.1.call-start = ((), (), s32[]{:S(2)}) async-start(), calls=%async_computation.15 | async-start | bytes 4718592 | tf_op jit(solution)/shard_map/all_gather | solution.py:28
  2080.5 17.0 copy-start.18
  2295.8 66.7 %copy-start.9 = (bf16[1024,256]{1,0:T(8,128)(2,1)S(1)}, bf16[1024,256]{1,0:T(8,128)(2,1)}, u32[]{:S(2)}) copy-start(bf16[1024,256]{1,0:T(8,128)(2,1)} %copy-done.2) | copy-start | bytes 1572868
  2295.8 66.7 %all-gather.53.cloned.1.call-start = ((), (), s32[]{:S(2)}) async-start(), calls=%async_computation.16 | async-start | bytes 2621440 | tf_op jit(solution)/shard_map/all_gather | solution.py:30
  2335.0 287.6 %all-gather.55.cloned.1.call-start = ((), (), s32[]{:S(2)}) async-start(), calls=%async_computation.17 | async-start | bytes 4718592 | tf_op jit(solution)/shard_map/all_gather | solution.py:28
  2380.5 17.0 copy-start.11
  2595.8 66.7 %copy-start.10 = (bf16[1024,256]{1,0:T(8,128)(2,1)S(1)}, bf16[1024,256]{1,0:T(8,128)(2,1)}, u32[]{:S(2)}) copy-start(bf16[1024,256]{1,0:T(8,128)(2,1)} %copy-done.2) | copy-start | bytes 1572868
  2595.8 66.7 %all-gather.57.cloned.1.call-start = ((), (), s32[]{:S(2)}) async-start(), calls=%async_computation.18 | async-start | bytes 2621440 | tf_op jit(solution)/shard_map/all_gather | solution.py:30
  (48 other events, 699.8 us)
Sparse Core Ops, SparseCore 0:
  10.2 33.8 all-gather.22
  45.7 151.6 all-gather.20
  209.8 30.6 all-gather.24
  496.4 26.2 all-gather.26
  535.3 27.3 all-gather.28
  796.1 26.6 all-gather.30
  835.3 27.3 all-gather.32
  1096.1 26.6 all-gather.34
  1135.3 27.3 all-gather.36
  1396.1 26.6 all-gather.38
  1435.3 27.3 all-gather.40
  1696.2 26.6 all-gather.42
  1735.4 27.3 all-gather.44
  1996.1 26.6 all-gather.46
  2035.3 27.3 all-gather.48
  2295.9 26.6 all-gather.50
  2335.1 27.3 all-gather.52
  2595.9 26.6 all-gather.54
  2635.2 27.3 all-gather.56
where the time goes:
time: 2730 us; the launch traced here: 2720 us
  blocking collectives  1890 us (69%)
  waiting for transfers between devices  590 us (22%)
  matrix products  133 us (5%)
  other arithmetic  73 us (3%)
    psum x80, blocking collectives, sweep(): lax.psum(jnp.sum(kernel * row_scale[:, None], axis=0), 'rows')  1180 us
    psum x80, blocking collectives, sweep(): lax.psum(jnp.sum(kernel * scales[1][None, :], axis=1), 'cols')  542 us
    all_gather x9, waiting for transfers between devices, cost_of(): lax.all_gather(plan_blk.astype(jnp.bfloat16), 'rows', axis=0, tiled=True)  218 us
    all_gather x9, waiting for transfers between devices, cost_of(): lax.all_gather(lead_blk.astype(jnp.bfloat16), 'cols', axis=1, tiled=True)  218 us
    all_gather x1, waiting for transfers between devices, local_fn(): lax.all_gather(c1_blk.astype(jnp.bfloat16), 'cols', axis=1, tiled=True)  153 us
    dot_general x9, matrix products, cost_of(): lead_blk = jnp.dot(c1_panel, plan_panel, preferred_element_type=jnp.float32)  111 us
  transfers between devices with their start and end apart: 19, of which 18 were waited for; matrix products, arithmetic and copies ran while one was open for 0% of the time, Pallas kernels for 0%

commit v1 on v0

v1 whole, which is shorter than its diff:
```python
import functools

import jax
import jax.numpy as jnp
from jax import lax
from jax.experimental import pallas as pl
from jax.experimental.pallas import tpu as pltpu
from jax.sharding import PartitionSpec as P

SWEEPS = 10
MESH = pl.DeviceIdType.MESH
BLK = 128


def gw_kernel(n_rows, n_cols, n_steps, eps_ref, c1_ref, c2_ref, t0_ref, p_ref, q_ref, a_ref, b_ref,
              t_ref, loss_ref, tp, ap, lead, cross, kern, u_ref, red,
              t_send, t_recv, a_send, a_recv, s_send, s_recv):
    me_r = lax.axis_index("rows")
    me_c = lax.axis_index("cols")
    chip, core = me_r // 2, me_r % 2
    n_chips = n_rows // 2
    height = t0_ref.shape[0]
    width = t0_ref.shape[1]
    half = height // 2

    def row_id(chip_off, core_sel):
        return ((chip + chip_off + n_chips) % n_chips) * 2 + core_sel

    sib = row_id(0, 1 - core)
    right, left = row_id(1, core), row_id(-1, core)
    up, down = (me_c + 1) % n_cols, (me_c + n_cols - 1) % n_cols

    barrier = pltpu.get_barrier_semaphore()
    for d in range(1, n_rows):
        pl.semaphore_signal(barrier, inc=1, device_id={"rows": (me_r + d) % n_rows}, device_id_type=MESH)
    for other in (up, down):
        pl.semaphore_signal(barrier, inc=1, device_id={"cols": other}, device_id_type=MESH)
    pl.semaphore_wait(barrier, n_rows + 1)

    def t_copy(slot, part, target, send_idx):
        ref = tp.at[slot, pl.ds(part * half, half)]
        return pltpu.make_async_remote_copy(src_ref=ref, dst_ref=ref, send_sem=t_send.at[send_idx],
                                            recv_sem=t_recv.at[slot, part], device_id={"rows": target}, device_id_type=MESH)

    def a_copy(par, slot, part, target, send_idx):
        ref = ap.at[par, slot, pl.ds(part * half, half)]
        return pltpu.make_async_remote_copy(src_ref=ref, dst_ref=ref, send_sem=a_send.at[send_idx],
                                            recv_sem=a_recv.at[par, slot, part], device_id={"cols": target}, device_id_type=MESH)

    def lead_add(slot, first):
        cols = pl.ds(pl.multiple_of(slot * height, height), height)
        prod = jnp.dot(c1_ref[:, cols], tp[slot], preferred_element_type=jnp.float32)
        if first:
            lead[...] = prod
        else:
            lead[...] += prod

    def cross_add(par, slot, first):
        rows = pl.ds(pl.multiple_of(slot * width, width), width)
        prod = jnp.dot(ap[par, slot], c2_ref[rows, :], preferred_element_type=jnp.float32)
        if first:
            cross[...] = prod
        else:
            cross[...] += prod

    def cost(step):
        sent = []

        def send(slot, part, target):
            copy = t_copy(slot, part, target, len(sent))
            copy.start()
            sent.append(copy)

        def recv(slot, part):
            t_copy(slot, part, sib, 0).wait_recv()

        for part in (0, 1):
            send(me_r, part, right)
            send(me_r, 1 - part, left)
        for part in (0, 1):
            send(me_r, part, sib)
        lead_add(me_r, True)
        recv(sib, 0)
        recv(sib, 1)
        lead_add(sib, False)
        recv(left, 0)
        send(left, 0, right)
        send(left, 0, sib)
        recv(right, 1)
        send(right, 1, left)
        send(right, 1, sib)
        recv(left, 1)
        send(left, 1, sib)
        recv(right, 0)
        send(right, 0, sib)
        lead_add(left, False)
        lead_add(right, False)
        for off in (-1, 1):
            slot = row_id(off, 1 - core)
            recv(slot, 0)
            recv(slot, 1)
            lead_add(slot, False)
        far = row_id(2, core)
        for part in (0, 1):
            recv(far, part)
            send(far, part, sib)
        lead_add(far, False)
        far_sib = row_id(2, 1 - core)
        recv(far_sib, 0)
        recv(far_sib, 1)
        lead_add(far_sib, False)
        for copy in sent:
            copy.wait_send()

        par = step % 2
        ap[par, me_c] = lead[...].astype(jnp.bfloat16)
        sent_a = []

        def send_a(slot, part, target):
            copy = a_copy(par, slot, part, target, len(sent_a))
            copy.start()
            sent_a.append(copy)

        def recv_a(slot, part):
            a_copy(par, slot, part, up, 0).wait_recv()

        for part in (0, 1):
            send_a(me_c, part, up)
            send_a(me_c, 1 - part, down)
        cross_add(par, me_c, True)
        recv_a(down, 0)
        send_a(down, 0, up)
        recv_a(up, 1)
        send_a(up, 1, down)
        recv_a(down, 1)
        cross_add(par, down, False)
        recv_a(up, 0)
        cross_add(par, up, False)
        opp = (me_c + 2) % n_cols
        recv_a(opp, 0)
        recv_a(opp, 1)
        cross_add(par, opp, False)
        for copy in sent_a:
            copy.wait_send()

    def group_sum(par, value):
        red[par, me_r] = value
        copies = []
        for d in range(1, n_rows):
            other = (me_r + d) % n_rows
            copy = pltpu.make_async_remote_copy(src_ref=red.at[par, me_r], dst_ref=red.at[par, me_r],
                                                send_sem=s_send.at[par, d - 1], recv_sem=s_recv.at[par, me_r],
                                                device_id={"rows": other}, device_id_type=MESH)
            copy.start()
            copies.append(copy)
        for d in range(1, n_rows):
            other = (me_r + d) % n_rows
            pltpu.make_async_remote_copy(src_ref=red.at[par, other], dst_ref=red.at[par, other],
                                         send_sem=s_send.at[par, d - 1], recv_sem=s_recv.at[par, other],
                                         device_id={"rows": other}, device_id_type=MESH).wait_recv()
        total = red[par, 0]
        for d in range(1, n_rows):
            total = total + red[par, d]
        for copy in copies:
            copy.wait_send()
        return total

    n_blk = height // BLK

    def fold(block):
        return jnp.sum(block.reshape(BLK // 8, 8, block.shape[1]), axis=0)

    def make_kernel(step):
        inv_eps = 1.0 / jnp.full((1, 1), eps_ref[step], jnp.float32)
        for k in range(n_blk):
            rows = pl.ds(k * BLK, BLK)
            block = (a_ref[rows, :] + b_ref[...]) - 2.0 * cross[rows, :]
            low = jnp.min(block, axis=1, keepdims=True)
            kern[rows, :] = jnp.exp((low - block) * inv_eps)

    def sweep(par, v):
        acc = jnp.zeros((8, v.shape[1]), jnp.float32)
        for k in range(n_blk):
            rows = pl.ds(k * BLK, BLK)
            u = p_ref[rows, :] / jnp.sum(kern[rows, :] * v, axis=1, keepdims=True)
            u_ref[rows, :] = u
            acc = acc + fold(kern[rows, :] * u)
        total = group_sum(par, jnp.sum(acc, axis=0, keepdims=True))
        return q_ref[...] / total

    my_cols = pl.ds(pl.multiple_of(me_c * width, width), width)
    v_ref = loss_ref

    def outer(step, carry):
        cost(step)

        @pl.when(step < n_steps)
        def _():
            make_kernel(step)

            def two_sweeps(i, v):
                return sweep(1, sweep(0, v))

            v = lax.fori_loop(0, SWEEPS // 2, two_sweeps, jnp.ones_like(q_ref))
            v_ref[...] = v
            for k in range(n_blk):
                rows = pl.ds(k * BLK, BLK)
                plan = u_ref[rows, :] * kern[rows, my_cols] * v_ref[:, my_cols]
                t_ref[rows, :] = plan
                tp[me_r, rows, :] = plan.astype(jnp.bfloat16)

        return carry

    tp[me_r] = t0_ref[...].astype(jnp.bfloat16)
    lax.fori_loop(0, n_steps + 1, outer, 0)

    v = v_ref[...]
    acc = jnp.zeros((8, v.shape[1]), jnp.float32)
    for k in range(n_blk):
        rows = pl.ds(k * BLK, BLK)
        block = (a_ref[rows, :] + b_ref[...]) - 2.0 * cross[rows, :]
        acc = acc + fold(block * (u_ref[rows, :] * kern[rows, :] * v))
    total = group_sum(0, jnp.sum(acc, axis=0, keepdims=True))
    loss_ref[...] = jnp.broadcast_to(jnp.sum(total, axis=1, keepdims=True), loss_ref.shape)


def solution(mesh):
    grid_spec = P(("pairs", "rows"), "cols")
    n_rows, n_cols = mesh.shape["rows"], mesh.shape["cols"]

    def local_fn(c1_blk, c2_blk, t0_blk, p_blk, q_blk, eps_blk):
        col_pos = lax.axis_index("cols")
        row_pos = lax.axis_index("rows")
        c1_width = c1_blk.shape[1]
        c2_height = c2_blk.shape[0]
        height, width = t0_blk.shape
        full = width * n_cols
        p_full = lax.all_gather(p_blk, "rows", tiled=True)
        q_full = lax.all_gather(q_blk, "cols", tiled=True)
        p_piece = lax.dynamic_slice_in_dim(p_full, col_pos * c1_width, c1_width)
        q_piece = lax.dynamic_slice_in_dim(q_full, row_pos * c2_height, c2_height)
        row_term = lax.psum(jnp.sum(c1_blk * c1_blk * p_piece[None, :], axis=1), "cols")
        col_blk = lax.psum(jnp.sum(c2_blk * c2_blk * q_piece[:, None], axis=0), "rows")
        col_term = lax.all_gather(col_blk, "cols", tiled=True)
        c1_panel = lax.all_gather(c1_blk.astype(jnp.bfloat16), "cols", axis=1, tiled=True)
        c2_panel = lax.all_gather(c2_blk.astype(jnp.bfloat16), "rows", axis=0, tiled=True)
        c2_full = lax.all_gather(c2_panel, "cols", axis=1, tiled=True)
        n_steps = eps_blk.shape[0]
        vmem = pl.BlockSpec(memory_space=pltpu.VMEM)
        f32, b16, dma = jnp.float32, jnp.bfloat16, pltpu.SemaphoreType.DMA
        plan, loss = pl.pallas_call(
            functools.partial(gw_kernel, n_rows, n_cols, n_steps),
            out_shape=(jax.ShapeDtypeStruct((height, width), f32), jax.ShapeDtypeStruct((1, full), f32)),
            in_specs=[pl.BlockSpec(memory_space=pltpu.SMEM)] + [vmem] * 7,
            out_specs=(vmem, vmem),
            scratch_shapes=[
                pltpu.VMEM((n_rows, height, width), b16),
                pltpu.VMEM((2, n_cols, height, width), b16),
                pltpu.VMEM((height, width), f32),
                pltpu.VMEM((height, full), f32),
                pltpu.VMEM((height, full), f32),
                pltpu.VMEM((height, 1), f32),
                pltpu.VMEM((2, n_rows, 1, full), f32),
                dma((14,)), dma((n_rows, 2)), dma((6,)), dma((2, n_cols, 2)),
                dma((2, n_rows - 1)), dma((2, n_rows)),
            ],
            compiler_params=pltpu.CompilerParams(collective_id=0, has_side_effects=True, vmem_limit_bytes=60 * 2**20),
        )(eps_blk, c1_panel, c2_full, t0_blk, p_blk[:, None], q_full[None, :], row_term[:, None], col_term[None, :])
        return plan, loss[0, :1]

    return jax.shard_map(local_fn, mesh=mesh, in_specs=(grid_spec, grid_spec, grid_spec, P(("pairs", "rows")), P(("pairs", "cols")), P("pairs")), out_specs=(grid_spec, P("pairs")), check_vma=False)
```

time: 2730 us -> 995 us (0.36)
  blocking collectives: 1890 us -> 105 us
  Pallas kernels: 0 us -> 747 us
  waiting for transfers between devices: 590 us -> 113 us
  matrix products: 133 us -> 0 us
  other arithmetic: 73 us -> 10.3 us
    psum x161 -> x0, blocking collectives: 1770 us -> none  [the longest x80 1180 us: sweep(): lax.psum(jnp.sum(kernel * row_scale[:, None], axis=0), 'rows')]
    pallas_call x0 -> x1, Pallas kernels: none -> 747 us  [local_fn(): pl.pallas_call(functools.partial(gw_kernel, n_rows, n_cols, n_steps), out...]
    all_gather x18 -> x1, waiting for transfers between devices: 435 us -> 0.01 us  [local_fn(): c2_full = lax.all_gather(c2_panel, 'cols', axis=1, tiled=True)]
    dot_general x18 -> x0, matrix products: 133 us -> none  [the longest x9 111 us: cost_of(): lead_blk = jnp.dot(c1_panel, plan_panel, preferred_element_type=jnp.float32)]
    pmin x8 -> x0, blocking collectives: 54.2 us -> none  [local_fn(): row_shift = lax.pmin(jnp.min(cost_blk, axis=1), 'cols')]
    all_gather x1, waiting for transfers between devices: 153 us -> 113 us  [local_fn(): lax.all_gather(c1_blk.astype(jnp.bfloat16), 'cols', axis=1, tiled=True)]
    reduce_sum x160 -> x0, other arithmetic: 34.5 us -> none  [the longest x80 17.7 us: sweep(): jnp.sum(kernel * row_scale[:, None], axis=0)]
  transfers between devices with their start and end apart: 19 -> 2, of which waited for: 18 -> 1; matrix products, arithmetic and copies ran while one was open for 0% -> 1% of each run, Pallas kernels for 0% -> 0%
where the time goes in v1:
time: 995 us; the launch traced here: 994 us
  Pallas kernels  747 us (75%)
  waiting for transfers between devices  113 us (11%)
  blocking collectives  105 us (11%)
  between operations  14.1 us (1%)
  other arithmetic  10.3 us (1%)
    pallas_call x1, Pallas kernels, local_fn(): pl.pallas_call(functools.partial(gw_kernel, n_rows, n_cols, n_steps), out...  747 us
    all_gather x1, waiting for transfers between devices, local_fn(): lax.all_gather(c1_blk.astype(jnp.bfloat16), 'cols', axis=1, tiled=True)  113 us
    psum x1, blocking collectives, local_fn(): lax.psum(jnp.sum(c1_blk * c1_blk * p_piece[None, :], axis=1), 'cols')  28.5 us
    all_gather x1, blocking collectives, local_fn(): p_full = lax.all_gather(p_blk, 'rows', tiled=True)  22.8 us
    all_gather x1, blocking collectives, local_fn(): lax.all_gather(c2_blk.astype(jnp.bfloat16), 'rows', axis=0, tiled=True)  20.1 us
  transfers between devices with their start and end apart: 2, of which 1 were waited for; matrix products, arithmetic and copies ran while one was open for 1% of the time, Pallas kernels for 0%

profile of v1, /device:TPU:97, one launch (start us, length us, event | category | flops | bytes accessed | tf_op | source)
XLA Modules:
  0.0 994.4 jit_solution(12970868362689314897)
XLA Ops:
  7.2 0.1 all-gather.7.cloned.1.call-start
  7.2 10.5 %all-gather = f32[4,1,256]{2,1,0:T(1,128)S(1)} all-gather(f32[1,1,256]{2,1,0:T(1,128)} %bitcast.14), channel_id=1, replica_groups=mesh['pairs'=1,'cols'=4,'rows'=8] {'cols'}, dimensions={0}, use_global_device_ids=true | all-gather | bytes 5120 | tf_op jit(solution)/shard_map/all_gather | solution.py:239
  17.7 0.0 copy-start.1
  17.7 0.1 dynamic_slice.7
  17.8 1.1 multiply_reduce_fusion.1
  18.9 20.1 %all_gather.19 = bf16[1024,256]{1,0:T(8,128)(2,1)} all-gather(bf16[128,256]{1,0:T(8,128)(2,1)S(1)} %get-tuple-element.9), channel_id=1, replica_groups=mesh['pairs'=1,'cols'=4,'rows'=8] {'rows'}, dimensions={0}, use_global_device_ids=true | all-gather | bytes 589824 | tf_op jit(solution)/shard_map/all_gather | solution.py:246
  39.0 0.1 all-gather.7.cloned.1.call-update
  39.1 0.1 all-gather.5.cloned.1.call-start
  39.2 22.8 %all_gather.22 = f32[8192]{0:T(1024)S(1)} all-gather(f32[1024]{0:T(1024)} %param.9), channel_id=1, replica_groups=mesh['pairs'=1,'cols'=4,'rows'=8] {'rows'}, dimensions={0}, use_global_device_ids=true | all-gather | bytes 36864 | tf_op jit(solution)/shard_map/all_gather | solution.py:238
  62.0 0.0 copy-start
  62.0 9.2 multiply_reduce_fusion
  71.2 0.1 all-gather.5.cloned.1.call-update
  71.3 0.0 copy-done.1
  71.3 0.0 copy-done
  71.3 1.0 copy.11.p_ref
  72.3 0.2 copy.10
  72.5 16.9 %psum.15 = f32[256]{0:T(256)S(1)} all-reduce(f32[256]{0:T(256)S(1)} %get-tuple-element.8), channel_id=1, replica_groups=mesh['pairs'=1,'cols'=4,'rows'=8] {'rows'}, use_global_device_ids=true, to_apply=%region_3.0 | all-reduce | flops 256 | bytes 2048 | tf_op jit(solution)/shard_map/psum | solution.py:243
  89.5 5.8 all-gather.1
  95.3 28.5 %psum.14.a_ref = f32[1024,1]{1,0:T(8,128)} all-reduce(f32[1024,1]{1,0:T(8,128)S(1)} %copy.10), channel_id=1, replica_groups=mesh['pairs'=1,'cols'=4,'rows'=8] {'cols'}, use_global_device_ids=true, to_apply=%region_1.0 | all-reduce | flops 1024 | bytes 8192 | tf_op jit(solution)/shard_map/psum | solution.py:242
  123.8 0.0 all-gather.7.cloned.1.call-done.c2_ref
  123.8 113.4 %all-gather.5.cloned.1.call-done.c1_ref = bf16[1024,8192]{1,0:T(8,128)(2,1)} async-done(((bf16[1024,2048]{1,0:T(8,128)(2,1)}), bf16[1024,8192]{1,0:T(8,128)(2,1)}) %all-gather.5.cloned.1.call-update) | async-done | bytes 16777232 | tf_op jit(solution)/shard_map/all_gather | solution.py:245
  237.1 747.0 %shard_map.77 = (f32[1024,256]{1,0:T(8,128)}, f32[1,1024]{1,0:T(1,128)}) custom-call(f32[8]{0:T(128)} %eps_ref.1, bf16[1024,8192]{1,0:T(8,128)(2,1)} %all-gather.5.cloned.1.call-done.c1_ref, bf16[1024,1024]{1,0:T(8,128)(2,1)} %all-gather.7.cloned.1.call-done.c2_ref, f32[1024,256]{1,0:T(8,128)} %t0_ref.1, f32[1024,1]{1,0:T(8,128)} %copy.11.p_ref, ...), custom_call_target="tpu_custom_call" | custom-call | tf_op jit(solution)/shard_map/pallas_call | solution.py:251
  984.2 1.1 slice.3
  985.3 2.3 copy.13
  (1 shorter events, 0.0 us)
Async XLA Ops:
  7.2 116.6 %all-gather.7.cloned.1.call-start = ((), (), s32[]{:S(2)}) async-start(), calls=%async_computation.1 | async-start | bytes 2621440 | tf_op jit(solution)/shard_map/all_gather | solution.py:247
  17.7 53.6 %copy-start.1 = (f32[4,1,256]{2,1,0:T(1,128)}, f32[4,1,256]{2,1,0:T(1,128)S(1)}, u32[]{:S(2)}) copy-start(f32[4,1,256]{2,1,0:T(1,128)S(1)} %all-gather) | copy-start | bytes 12292
  39.1 198.1 %all-gather.5.cloned.1.call-start = ((), (), s32[]{:S(2)}) async-start(), calls=%async_computation | async-start | bytes 20971520 | tf_op jit(solution)/shard_map/all_gather | solution.py:245
  62.0 9.3 copy-start
Sparse Core Ops, SparseCore 0:
  39.2 32.9 all-gather.6
  73.8 163.2 all-gather.4

commit v2 on v0

v2 whole, which is shorter than its diff:
```python
import functools

import jax
import jax.numpy as jnp
from jax import lax
from jax.experimental import pallas as pl
from jax.experimental.pallas import tpu as pltpu
from jax.sharding import PartitionSpec as P

SWEEPS = 10
MESH = pl.DeviceIdType.MESH
BLK = 128
LANES = 128
PIECE = 256


def gw_kernel(n_rows, n_cols, n_steps, eps_ref, c1_ref, c2_ref, t0_ref, p_ref, q_ref,
              t_ref, loss_ref, c1s, tp, ap, lead, cross, kern, u_ref, red,
              stage, a_acc, a_col, p_col, b_row, q_row, c2f, c2s, p_all, q_all, b_all, b_red, a_red,
              t_send, t_recv, a_send, a_recv, s_send, s_recv, c_send, c_recv, x_send, x_recv, ld_sem):
    me_r = lax.axis_index("rows")
    me_c = lax.axis_index("cols")
    chip, core = me_r // 2, me_r % 2
    n_chips = n_rows // 2
    height, width = t0_ref.shape
    half = height // 2
    n_chunk = width // LANES
    n_piece = c1_ref.shape[1] // PIECE
    per_slot = height // PIECE
    n_blk = height // BLK

    def row_id(chip_off, core_sel):
        return ((chip + chip_off + n_chips) % n_chips) * 2 + core_sel

    sib = row_id(0, 1 - core)
    right, left, far = row_id(1, core), row_id(-1, core), row_id(2, core)
    up, down, opp = (me_c + 1) % n_cols, (me_c + n_cols - 1) % n_cols, (me_c + 2) % n_cols

    barrier = pltpu.get_barrier_semaphore()
    for d in range(1, n_rows):
        pl.semaphore_signal(barrier, inc=1, device_id={"rows": (me_r + d) % n_rows}, device_id_type=MESH)
    for d in range(1, n_cols):
        pl.semaphore_signal(barrier, inc=1, device_id={"cols": (me_c + d) % n_cols}, device_id_type=MESH)
    pl.semaphore_wait(barrier, n_rows + n_cols - 2)

    def share(idx, axis, ref_of):
        me, n = (me_r, n_rows) if axis == "rows" else (me_c, n_cols)

        def copy(slot, d):
            return pltpu.make_async_remote_copy(src_ref=ref_of(slot), dst_ref=ref_of(slot), send_sem=x_send.at[idx, d],
                                                recv_sem=x_recv.at[idx, slot], device_id={axis: (me + d) % n}, device_id_type=MESH)

        for d in range(1, n):
            copy(me, d).start()

        def finish():
            for d in range(1, n):
                copy((me + d) % n, d).wait_recv()
            for d in range(1, n):
                copy(me, d).wait_send()

        return finish

    def group_sum(par, value):
        red[par, me_r] = value
        copies = []
        for d in range(1, n_rows):
            other = (me_r + d) % n_rows
            copy = pltpu.make_async_remote_copy(src_ref=red.at[par, me_r], dst_ref=red.at[par, me_r],
                                                send_sem=s_send.at[par, d - 1], recv_sem=s_recv.at[par, me_r],
                                                device_id={"rows": other}, device_id_type=MESH)
            copy.start()
            copies.append(copy)
        for d in range(1, n_rows):
            other = (me_r + d) % n_rows
            pltpu.make_async_remote_copy(src_ref=red.at[par, other], dst_ref=red.at[par, other],
                                         send_sem=s_send.at[par, d - 1], recv_sem=s_recv.at[par, other],
                                         device_id={"rows": other}, device_id_type=MESH).wait_recv()
        total = red[par, 0]
        for d in range(1, n_rows):
            total = total + red[par, d]
        for copy in copies:
            copy.wait_send()
        return total

    def t_copy(slot, chunk, part, target, send_idx):
        ref = tp.at[slot, chunk, pl.ds(part * half, half)]
        return pltpu.make_async_remote_copy(src_ref=ref, dst_ref=ref, send_sem=t_send.at[chunk, send_idx],
                                            recv_sem=t_recv.at[slot, chunk, part], device_id={"rows": target}, device_id_type=MESH)

    t_sent = []

    def t_push(slot, chunk, part, target, send_idx):
        copy = t_copy(slot, chunk, part, target, send_idx)
        copy.start()
        t_sent.append(copy)

    def t_take(slot, chunk, part):
        t_copy(slot, chunk, part, sib, 0).wait_recv()

    def t_start(chunk):
        for part in (0, 1):
            t_push(me_r, chunk, part, right, part)
            t_push(me_r, chunk, 1 - part, left, 2 + part)
        for part in (0, 1):
            t_push(me_r, chunk, part, sib, 4 + part)

    def t_near(chunk):
        t_take(left, chunk, 0)
        t_push(left, chunk, 0, right, 6)
        t_take(right, chunk, 1)
        t_push(right, chunk, 1, left, 7)
        t_push(left, chunk, 0, sib, 8)
        t_push(right, chunk, 1, sib, 9)

    def t_rest(chunk):
        t_take(left, chunk, 1)
        t_push(left, chunk, 1, sib, 10)
        t_take(right, chunk, 0)
        t_push(right, chunk, 0, sib, 11)

    def t_far(chunk):
        for part in (0, 1):
            t_take(far, chunk, part)
            t_push(far, chunk, part, sib, 12 + part)

    def t_sib(chunk, chip_off):
        slot = row_id(chip_off, 1 - core)
        t_take(slot, chunk, 0)
        t_take(slot, chunk, 1)
        return slot

    def t_done():
        for copy in t_sent:
            copy.wait_send()
        t_sent.clear()

    def a_copy(par, slot, chunk, part, target, send_idx):
        ref = ap.at[par, slot, chunk, pl.ds(part * half, half)]
        return pltpu.make_async_remote_copy(src_ref=ref, dst_ref=ref, send_sem=a_send.at[chunk, send_idx],
                                            recv_sem=a_recv.at[par, slot, chunk, part], device_id={"cols": target}, device_id_type=MESH)

    a_sent = []

    def a_push(par, slot, chunk, part, target, send_idx):
        copy = a_copy(par, slot, chunk, part, target, send_idx)
        copy.start()
        a_sent.append(copy)

    def a_take(par, slot, chunk, part):
        a_copy(par, slot, chunk, part, up, 0).wait_recv()

    def a_start(par, chunk):
        ap[par, me_c, chunk] = lead[chunk].astype(jnp.bfloat16)
        for part in (0, 1):
            a_push(par, me_c, chunk, part, up, part)
            a_push(par, me_c, chunk, 1 - part, down, 2 + part)

    def a_near(par, chunk):
        a_take(par, down, chunk, 0)
        a_push(par, down, chunk, 0, up, 4)
        a_take(par, up, chunk, 1)
        a_push(par, up, chunk, 1, down, 5)

    def a_rest(par, chunk):
        a_take(par, down, chunk, 1)
        a_take(par, up, chunk, 0)

    def a_far(par, chunk):
        a_take(par, opp, chunk, 0)
        a_take(par, opp, chunk, 1)

    def a_done():
        for copy in a_sent:
            copy.wait_send()
        a_sent.clear()

    def c1_slot(slot):
        return jnp.concatenate([c1s[slot * per_slot + j] for j in range(per_slot)], axis=1)

    def lead_add(slot, chunk, first=False):
        prod = jnp.dot(c1_slot(slot), tp[slot, chunk], preferred_element_type=jnp.float32)
        lead[chunk] = prod if first else lead[chunk] + prod

    def lead_both(slot):
        plan = jnp.concatenate([tp[slot, k] for k in range(n_chunk)], axis=1)
        prod = jnp.dot(c1_slot(slot), plan, preferred_element_type=jnp.float32)
        for k in range(n_chunk):
            lead[k] = lead[k] + prod[:, k * LANES:(k + 1) * LANES]

    def cross_add(par, slot, first=False):
        rows = pl.ds(pl.multiple_of(slot * width, width), width)
        block = jnp.concatenate([ap[par, slot, k] for k in range(n_chunk)], axis=1)
        prod = jnp.dot(block, c2s[rows, :], preferred_element_type=jnp.float32)
        cross[...] = prod if first else cross[...] + prod

    def cross_all(par):
        cross_add(par, me_c, True)

    def piece_load(i):
        cols = pl.ds(pl.multiple_of(i * PIECE, PIECE), PIECE)
        return pltpu.make_async_copy(c1_ref.at[:, cols], stage.at[i % 2], ld_sem.at[i % 2])

    def piece_copy(piece, target, send_idx):
        return pltpu.make_async_remote_copy(src_ref=c1s.at[piece], dst_ref=c1s.at[piece], send_sem=c_send.at[send_idx],
                                            recv_sem=c_recv.at[piece], device_id={"cols": target}, device_id_type=MESH)

    def prologue():
        piece_load(0).start()
        p_all[me_r] = p_ref[...]
        p_fin = share(0, "rows", lambda s: p_all.at[s])
        q_all[me_c] = q_ref[...]
        q_fin = share(1, "cols", lambda s: q_all.at[s])
        c2f[me_r, me_c] = c2_ref[...].astype(jnp.bfloat16)
        c2y_fin = share(2, "cols", lambda s: c2f.at[me_r, s])
        for k in range(n_chunk):
            tp[me_r, k] = t0_ref[:, k * LANES:(k + 1) * LANES].astype(jnp.bfloat16)
        for k in range(n_chunk):
            t_start(k)
        a_acc[...] = jnp.zeros_like(a_acc)
        p_fin()

        def own_piece(i, carry):
            piece_load(i).wait()

            @pl.when(i + 1 < n_piece)
            def _():
                piece_load(i + 1).start()

            block = stage[i % 2]
            piece = me_c * n_piece + i
            c1s[piece] = block.astype(jnp.bfloat16)
            piece_copy(piece, up, i).start()
            piece_copy(piece, down, n_piece + i).start()
            where = piece * PIECE
            p_row = p_all[where // height, :, pl.ds(pl.multiple_of(where % height, PIECE), PIECE)]
            sq = block * block * p_row
            acc = a_acc[...]
            for k in range(PIECE // LANES):
                acc = acc + sq[:, k * LANES:(k + 1) * LANES]
            a_acc[...] = acc
            return carry

        lax.fori_loop(0, n_piece, own_piece, 0)
        q_fin()
        q_row[...] = jnp.concatenate([q_all[k] for k in range(n_cols)], axis=1)
        a_red[me_c] = jnp.sum(a_acc[...].T, axis=0, keepdims=True)
        a_fin = share(3, "cols", lambda s: a_red.at[s])
        low = me_r * c2_ref.shape[0]
        q_piece = q_all[low // width, :, pl.ds(pl.multiple_of(low % width, LANES), LANES)]
        q_col = jnp.broadcast_to(q_piece, (LANES, LANES)).T
        sq = c2_ref[...] * c2_ref[...]
        b_red[me_r] = jnp.sum(sq * q_col[:, :1], axis=0, keepdims=True)
        b_fin = share(4, "rows", lambda s: b_red.at[s])
        p_col[...] = jnp.broadcast_to(p_ref[...], (LANES, height)).T[:, :1]
        c2y_fin()
        c2x_fin = share(5, "rows", lambda s: c2f.at[s])
        for k in range(n_chunk):
            t_near(k)
        for k in range(n_chunk):
            t_rest(k)
        b_fin()
        total = b_red[0]
        for s in range(1, n_rows):
            total = total + b_red[s]
        b_all[me_c] = total
        ball_fin = share(6, "cols", lambda s: b_all.at[s])
        for k in range(n_chunk):
            t_far(k)
        for k in range(n_chunk):
            for off in (0, -1, 1, 2):
                t_sib(k, off)
        t_done()
        lead[...] = jnp.zeros_like(lead)

        def group(which):
            def body(j, carry):
                lead_both(which * (n_piece // per_slot) + j)
                return carry

            lax.fori_loop(0, n_piece // per_slot, body, 0)

        group(me_c)
        hop = n_piece // 2
        for i in range(n_piece):
            piece_copy(down * n_piece + i, up, 0).wait_recv()
            if i < hop:
                piece_copy(down * n_piece + i, up, 2 * n_piece + i).start()
            piece_copy(up * n_piece + i, up, 0).wait_recv()
            if i >= hop:
                piece_copy(up * n_piece + i, down, 2 * n_piece + i).start()
        group(down)
        group(up)
        a_fin()
        total = a_red[0]
        for s in range(1, n_cols):
            total = total + a_red[s]
        a_col[...] = jnp.broadcast_to(total, (LANES, height)).T[:, :1]
        ball_fin()
        b_row[...] = jnp.concatenate([b_all[k] for k in range(n_cols)], axis=1)
        c2x_fin()
        depth = c2_ref.shape[0]
        for r in range(n_rows):
            for c in range(n_cols):
                c2s[r * depth:(r + 1) * depth, c * width:(c + 1) * width] = c2f[r, c]
        for i in range(n_piece):
            piece_copy(opp * n_piece + i, up, 0).wait_recv()
        group(opp)
        for i in range(n_piece):
            piece_copy(me_c * n_piece + i, up, i).wait_send()
            piece_copy(me_c * n_piece + i, down, n_piece + i).wait_send()
            if i < hop:
                piece_copy(down * n_piece + i, up, 2 * n_piece + i).wait_send()
            else:
                piece_copy(up * n_piece + i, down, 2 * n_piece + i).wait_send()

        for k in range(n_chunk):
            a_start(0, k)
        cross_add(0, me_c, True)
        for k in range(n_chunk):
            a_near(0, k)
        for k in range(n_chunk):
            a_rest(0, k)
        cross_add(0, down)
        cross_add(0, up)
        for k in range(n_chunk):
            a_far(0, k)
        cross_add(0, opp)
        a_done()

    def cost(par):
        def early(chunk):
            lead_add(me_r, chunk, True)
            lead_add(t_sib(chunk, 0), chunk)

        def middle(chunk):
            t_rest(chunk)
            lead_add(left, chunk)
            lead_add(right, chunk)
            lead_add(t_sib(chunk, -1), chunk)
            lead_add(t_sib(chunk, 1), chunk)

        def late(chunk):
            t_far(chunk)
            lead_add(far, chunk)
            lead_add(t_sib(chunk, 2), chunk)
            a_start(par, chunk)

        t_start(0)
        early(0)
        t_near(0)
        t_start(1)
        middle(0)
        early(1)
        late(0)
        t_near(1)
        middle(1)
        a_near(par, 0)
        late(1)
        a_rest(par, 0)
        cross_add(par, me_c, True)
        a_near(par, 1)
        a_rest(par, 1)
        cross_add(par, down)
        cross_add(par, up)
        a_far(par, 0)
        a_far(par, 1)
        cross_add(par, opp)
        t_done()
        a_done()

    def fold(block):
        return jnp.sum(block.reshape(BLK // 8, 8, block.shape[1]), axis=0)

    def make_kernel(step):
        inv_eps = 1.0 / jnp.full((1, 1), eps_ref[step], jnp.float32)
        for k in range(n_blk):
            rows = pl.ds(k * BLK, BLK)
            block = (a_col[rows, :] + b_row[...]) - 2.0 * cross[rows, :]
            low = jnp.min(block, axis=1, keepdims=True)
            kern[rows, :] = jnp.exp((low - block) * inv_eps)

    def sweep(par, v):
        acc = jnp.zeros((8, v.shape[1]), jnp.float32)
        for k in range(n_blk):
            rows = pl.ds(k * BLK, BLK)
            u = p_col[rows, :] / jnp.sum(kern[rows, :] * v, axis=1, keepdims=True)
            u_ref[rows, :] = u
            acc = acc + fold(kern[rows, :] * u)
        total = group_sum(par, jnp.sum(acc, axis=0, keepdims=True))
        return q_row[...] / total

    v_ref = loss_ref

    def outer(step, carry):
        make_kernel(step)

        def two_sweeps(i, v):
            return sweep(1, sweep(0, v))

        v_ref[...] = lax.fori_loop(0, SWEEPS // 2, two_sweeps, jnp.ones_like(q_row))
        for c in range(n_chunk):
            cols = pl.ds(pl.multiple_of(me_c * width + c * LANES, LANES), LANES)
            for k in range(n_blk):
                rows = pl.ds(k * BLK, BLK)
                plan = u_ref[rows, :] * kern[rows, cols] * v_ref[:, cols]
                t_ref[rows, c * LANES:(c + 1) * LANES] = plan
                tp[me_r, c, rows, :] = plan.astype(jnp.bfloat16)
        cost((step + 1) % 2)
        return carry

    prologue()
    lax.fori_loop(0, n_steps, outer, 0)

    v = v_ref[...]
    acc = jnp.zeros((8, v.shape[1]), jnp.float32)
    for k in range(n_blk):
        rows = pl.ds(k * BLK, BLK)
        block = (a_col[rows, :] + b_row[...]) - 2.0 * cross[rows, :]
        acc = acc + fold(block * (u_ref[rows, :] * kern[rows, :] * v))
    total = group_sum(0, jnp.sum(acc, axis=0, keepdims=True))
    loss_ref[...] = jnp.broadcast_to(jnp.sum(total, axis=1, keepdims=True), loss_ref.shape)


def solution(mesh):
    grid_spec = P(("pairs", "rows"), "cols")
    n_rows, n_cols = mesh.shape["rows"], mesh.shape["cols"]

    def local_fn(c1_blk, c2_blk, t0_blk, p_blk, q_blk, eps_blk):
        height, width = t0_blk.shape
        full = width * n_cols
        n_chunk = width // LANES
        n_piece = c1_blk.shape[1] // PIECE
        n_steps = eps_blk.shape[0]
        vmem = pl.BlockSpec(memory_space=pltpu.VMEM)
        f32, b16, dma = jnp.float32, jnp.bfloat16, pltpu.SemaphoreType.DMA
        plan, loss = pl.pallas_call(
            functools.partial(gw_kernel, n_rows, n_cols, n_steps),
            out_shape=(jax.ShapeDtypeStruct((height, width), f32), jax.ShapeDtypeStruct((1, full), f32)),
            in_specs=[pl.BlockSpec(memory_space=pltpu.SMEM), pl.BlockSpec(memory_space=pl.ANY)] + [vmem] * 4,
            out_specs=(vmem, vmem),
            scratch_shapes=[
                pltpu.VMEM((n_cols * n_piece, height, PIECE), b16),
                pltpu.VMEM((n_rows, n_chunk, height, LANES), b16),
                pltpu.VMEM((2, n_cols, n_chunk, height, LANES), b16),
                pltpu.VMEM((n_chunk, height, LANES), f32),
                pltpu.VMEM((height, full), f32),
                pltpu.VMEM((height, full), f32),
                pltpu.VMEM((height, 1), f32),
                pltpu.VMEM((2, n_rows, 1, full), f32),
                pltpu.VMEM((2, height, PIECE), f32),
                pltpu.VMEM((height, LANES), f32),
                pltpu.VMEM((height, 1), f32),
                pltpu.VMEM((height, 1), f32),
                pltpu.VMEM((1, full), f32),
                pltpu.VMEM((1, full), f32),
                pltpu.VMEM((n_rows, n_cols) + c2_blk.shape, b16),
                pltpu.VMEM((full, full), b16),
                pltpu.VMEM((n_rows, 1, height), f32),
                pltpu.VMEM((n_cols, 1, width), f32),
                pltpu.VMEM((n_cols, 1, width), f32),
                pltpu.VMEM((n_rows, 1, width), f32),
                pltpu.VMEM((n_cols, 1, height), f32),
                dma((n_chunk, 14)), dma((n_rows, n_chunk, 2)),
                dma((n_chunk, 6)), dma((2, n_cols, n_chunk, 2)),
                dma((2, n_rows - 1)), dma((2, n_rows)),
                dma((3 * n_piece,)), dma((n_cols * n_piece,)),
                dma((7, n_rows)), dma((7, n_rows)), dma((2,)),
            ],
            compiler_params=pltpu.CompilerParams(collective_id=0, has_side_effects=True, vmem_limit_bytes=62 * 2**20),
        )(eps_blk, c1_blk, c2_blk, t0_blk, p_blk[None, :], q_blk[None, :])
        return plan, loss[0, :1]

    return jax.shard_map(local_fn, mesh=mesh, in_specs=(grid_spec, grid_spec, grid_spec, P(("pairs", "rows")), P(("pairs", "cols")), P("pairs")), out_specs=(grid_spec, P("pairs")), check_vma=False)
```

time: 2730 us -> 828 us (0.30)
  blocking collectives: 1890 us -> 0 us
  Pallas kernels: 0 us -> 823 us
  waiting for transfers between devices: 590 us -> 0 us
  matrix products: 133 us -> 0 us
  other arithmetic: 73 us -> 0 us
    psum x163 -> x0, blocking collectives: 1790 us -> none  [the longest x80 1180 us: sweep(): lax.psum(jnp.sum(kernel * row_scale[:, None], axis=0), 'rows')]
    pallas_call x0 -> x1, Pallas kernels: none -> 823 us  [local_fn(): pl.pallas_call(functools.partial(gw_kernel, n_rows, n_cols, n_steps), out...]
    all_gather x19 -> x0, waiting for transfers between devices: 589 us -> none  [the longest x9 218 us: cost_of(): lax.all_gather(plan_blk.astype(jnp.bfloat16), 'rows', axis=0, tiled=True)]
    dot_general x18 -> x0, matrix products: 133 us -> none  [the longest x9 111 us: cost_of(): lead_blk = jnp.dot(c1_panel, plan_panel, preferred_element_type=jnp.float32)]
    pmin x8 -> x0, blocking collectives: 54.2 us -> none  [local_fn(): row_shift = lax.pmin(jnp.min(cost_blk, axis=1), 'cols')]
    all_gather x3 -> x0, blocking collectives: 44.4 us -> none  [the longest x1 19.9 us: local_fn(): p_full = lax.all_gather(p_blk, 'rows', tiled=True)]
    reduce_sum x162 -> x0, other arithmetic: 43.8 us -> none  [the longest x80 17.7 us: sweep(): jnp.sum(kernel * row_scale[:, None], axis=0)]
  transfers between devices with their start and end apart: 19 -> 0, of which waited for: 18 -> 0; matrix products, arithmetic and copies ran while one was open for 0% -> 0% of each run, Pallas kernels for 0% -> 0%
where the time goes in v2:
time: 828 us; the launch traced here: 827 us
  Pallas kernels  823 us (99%)
    pallas_call x1, Pallas kernels, local_fn(): pl.pallas_call(functools.partial(gw_kernel, n_rows, n_cols, n_steps), out...  823 us

profile of v2, /device:TPU:97, one launch (start us, length us, event | category | flops | bytes accessed | tf_op | source)
XLA Modules:
  0.0 827.3 jit_solution(10685079481798189399)
XLA Ops:
  0.6 823.3 %shard_map.77 = (f32[1024,256]{1,0:T(8,128)}, f32[1,1024]{1,0:T(1,128)}) custom-call(f32[8]{0:T(128)} %eps_ref.1, f32[1024,2048]{1,0:T(8,128)} %c1_ref.1, f32[128,256]{1,0:T(8,128)} %c2_ref.1, f32[1024,256]{1,0:T(8,128)} %t0_ref.1, f32[1,1024]{1,0:T(1,128)} %bitcast.3, f32[1,256]{1,0:T(1,128)} %bitcast.4), custom_call_target="tpu_custom_call" | custom-call | tf_op jit(solution)/shard_map/pallas_call | solution.py:437
  823.9 1.1 slice.3
  825.0 2.3 copy.9

commit v3 on v2

--- a/solution.py
+++ b/solution.py
@@ -12,10 +12,11 @@
 BLK = 128
 LANES = 128
 PIECE = 256
-
-
-def gw_kernel(n_rows, n_cols, n_steps, eps_ref, c1_ref, c2_ref, t0_ref, p_ref, q_ref,
-              t_ref, loss_ref, c1s, tp, ap, lead, cross, kern, u_ref, red,
+N_PART = 1
+
+
+def gw_kernel(n_rows, n_cols, n_steps, n_part, eps_ref, c1_ref, c2_ref, t0_ref, p_ref, q_ref,
+              t_ref, loss_ref, c1s, tp, ap, lead, cross, kern, u_ref, row_sum, red,
               stage, a_acc, a_col, p_col, b_row, q_row, c2f, c2s, p_all, q_all, b_all, b_red, a_red,
               t_send, t_recv, a_send, a_recv, s_send, s_recv, c_send, c_recv, x_send, x_recv, ld_sem):
     me_r = lax.axis_index("rows")
@@ -61,26 +62,24 @@
 
         return finish
 
-    def group_sum(par, value):
-        red[par, me_r] = value
-        copies = []
+    part_w = kern.shape[1] // n_part
+
+    def sum_copy(par, h, ref, d):
+        return pltpu.make_async_remote_copy(src_ref=ref, dst_ref=ref, send_sem=s_send.at[par, h], recv_sem=s_recv.at[par, h],
+                                            device_id={"rows": (me_r + d) % n_rows}, device_id_type=MESH)
+
+    def push(par, h, value):
+        red[par, h, me_r] = value
         for d in range(1, n_rows):
-            other = (me_r + d) % n_rows
-            copy = pltpu.make_async_remote_copy(src_ref=red.at[par, me_r], dst_ref=red.at[par, me_r],
-                                                send_sem=s_send.at[par, d - 1], recv_sem=s_recv.at[par, me_r],
-                                                device_id={"rows": other}, device_id_type=MESH)
-            copy.start()
-            copies.append(copy)
+            sum_copy(par, h, red.at[par, h, me_r], d).start()
+
+    def pull(par, h):
+        every = sum_copy(par, h, red.at[par, h, pl.ds(0, n_rows - 1)], 1)
+        every.wait_recv()
+        total = red[par, h, 0]
         for d in range(1, n_rows):
-            other = (me_r + d) % n_rows
-            pltpu.make_async_remote_copy(src_ref=red.at[par, other], dst_ref=red.at[par, other],
-                                         send_sem=s_send.at[par, d - 1], recv_sem=s_recv.at[par, other],
-                                         device_id={"rows": other}, device_id_type=MESH).wait_recv()
-        total = red[par, 0]
-        for d in range(1, n_rows):
-            total = total + red[par, d]
-        for copy in copies:
-            copy.wait_send()
+            total = total + red[par, h, d]
+        every.wait_send()
         return total
 
     def t_copy(slot, chunk, part, target, send_idx):
@@ -178,8 +177,13 @@
     def c1_slot(slot):
         return jnp.concatenate([c1s[slot * per_slot + j] for j in range(per_slot)], axis=1)
 
-    def lead_add(slot, chunk, first=False):
-        prod = jnp.dot(c1_slot(slot), tp[slot, chunk], preferred_element_type=jnp.float32)
+    def lead_add(slot, chunk, part=None, first=False):
+        if part is None:
+            prod = jnp.dot(c1_slot(slot), tp[slot, chunk], preferred_element_type=jnp.float32)
+        else:
+            hop = per_slot // 2
+            block = jnp.concatenate([c1s[slot * per_slot + part * hop + j] for j in range(hop)], axis=1)
+            prod = jnp.dot(block, tp[slot, chunk, part * half:(part + 1) * half], preferred_element_type=jnp.float32)
         lead[chunk] = prod if first else lead[chunk] + prod
 
     def lead_both(slot):
@@ -188,14 +192,15 @@
         for k in range(n_chunk):
             lead[k] = lead[k] + prod[:, k * LANES:(k + 1) * LANES]
 
-    def cross_add(par, slot, first=False):
-        rows = pl.ds(pl.multiple_of(slot * width, width), width)
-        block = jnp.concatenate([ap[par, slot, k] for k in range(n_chunk)], axis=1)
-        prod = jnp.dot(block, c2s[rows, :], preferred_element_type=jnp.float32)
+    def cross_add(par, pairs, first=False):
+        block = jnp.concatenate([ap[par, slot, k] for slot, k in pairs], axis=1)
+        rows = [pl.ds(pl.multiple_of(slot * width + k * LANES, LANES), LANES) for slot, k in pairs]
+        right_side = jnp.concatenate([c2s[r, :] for r in rows], axis=0)
+        prod = jnp.dot(block, right_side, preferred_element_type=jnp.float32)
         cross[...] = prod if first else cross[...] + prod
 
-    def cross_all(par):
-        cross_add(par, me_c, True)
+    def whole(slot):
+        return [(slot, k) for k in range(n_chunk)]
 
     def piece_load(i):
         cols = pl.ds(pl.multiple_of(i * PIECE, PIECE), PIECE)
@@ -316,29 +321,36 @@
 
         for k in range(n_chunk):
             a_start(0, k)
-        cross_add(0, me_c, True)
+        cross_add(0, whole(me_c), True)
         for k in range(n_chunk):
             a_near(0, k)
         for k in range(n_chunk):
             a_rest(0, k)
-        cross_add(0, down)
-        cross_add(0, up)
+        cross_add(0, whole(down))
+        cross_add(0, whole(up))
         for k in range(n_chunk):
             a_far(0, k)
-        cross_add(0, opp)
+        cross_add(0, whole(opp))
         a_done()
 
+    def t_sib_part(chunk, chip_off, part):
+        slot = row_id(chip_off, 1 - core)
+        t_take(slot, chunk, part)
+        lead_add(slot, chunk, part)
+
     def cost(par):
-        def early(chunk):
-            lead_add(me_r, chunk, True)
-            lead_add(t_sib(chunk, 0), chunk)
-
-        def middle(chunk):
+        def near(chunk):
+            lead_add(left, chunk, 0)
+            lead_add(right, chunk, 1)
+            t_sib_part(chunk, -1, 0)
+            t_sib_part(chunk, 1, 1)
+
+        def rest(chunk):
             t_rest(chunk)
-            lead_add(left, chunk)
-            lead_add(right, chunk)
-            lead_add(t_sib(chunk, -1), chunk)
-            lead_add(t_sib(chunk, 1), chunk)
+            lead_add(left, chunk, 1)
+            lead_add(right, chunk, 0)
+            t_sib_part(chunk, -1, 1)
+            t_sib_part(chunk, 1, 0)
 
         def late(chunk):
             t_far(chunk)
@@ -346,59 +358,98 @@
             lead_add(t_sib(chunk, 2), chunk)
             a_start(par, chunk)
 
-        t_start(0)
-        early(0)
+        lead_add(me_r, 0, None, True)
+        lead_add(t_sib(0, 0), 0)
         t_near(0)
         t_start(1)
-        middle(0)
-        early(1)
+        near(0)
+        lead_add(me_r, 1, None, True)
+        lead_add(t_sib(1, 0), 1)
+        rest(0)
         late(0)
         t_near(1)
-        middle(1)
+        near(1)
+        rest(1)
         a_near(par, 0)
         late(1)
         a_rest(par, 0)
-        cross_add(par, me_c, True)
+        cross_add(par, whole(me_c), True)
+        cross_add(par, [(down, 0), (up, 0)])
+        a_far(par, 0)
+        cross_add(par, [(opp, 0)])
         a_near(par, 1)
         a_rest(par, 1)
-        cross_add(par, down)
-        cross_add(par, up)
-        a_far(par, 0)
+        cross_add(par, [(down, 1), (up, 1)])
         a_far(par, 1)
-        cross_add(par, opp)
+        cross_add(par, [(opp, 1)])
         t_done()
         a_done()
 
     def fold(block):
         return jnp.sum(block.reshape(BLK // 8, 8, block.shape[1]), axis=0)
 
-    def make_kernel(step):
+    def part_cols(h):
+        return slice(h * part_w, (h + 1) * part_w)
+
+    def row_lanes(block, weight):
+        total = None
+        for j in range(block.shape[1] // LANES):
+            cols = slice(j * LANES, (j + 1) * LANES)
+            term = block[:, cols] if weight is None else block[:, cols] * weight[:, cols]
+            total = term if total is None else total + term
+        return total
+
+    def push_part(par, h):
+        acc = jnp.zeros((8, part_w), jnp.float32)
+        for k in range(n_blk):
+            rows = pl.ds(k * BLK, BLK)
+            acc = acc + fold(kern[rows, part_cols(h)] * u_ref[rows, :])
+        push(par, h, jnp.sum(acc, axis=0, keepdims=True))
+
+    def first_sweep(step):
         inv_eps = 1.0 / jnp.full((1, 1), eps_ref[step], jnp.float32)
         for k in range(n_blk):
             rows = pl.ds(k * BLK, BLK)
             block = (a_col[rows, :] + b_row[...]) - 2.0 * cross[rows, :]
             low = jnp.min(block, axis=1, keepdims=True)
-            kern[rows, :] = jnp.exp((low - block) * inv_eps)
-
-    def sweep(par, v):
-        acc = jnp.zeros((8, v.shape[1]), jnp.float32)
+            block = jnp.exp((low - block) * inv_eps)
+            kern[rows, :] = block
+            u_ref[rows, :] = p_col[rows, :] / jnp.sum(row_lanes(block, None), axis=1, keepdims=True)
+        for h in range(n_part):
+            push_part(0, h)
+
+    def scale(par, h):
+        return q_row[:, part_cols(h)] / pull(par, h)
+
+    def sweep(i, carry):
+        prev, cur = (i + 1) % 2, i % 2
+        for h in range(n_part - 1):
+            v = scale(prev, h)
+            for k in range(n_blk):
+                rows = pl.ds(k * BLK, BLK)
+                lanes = row_lanes(kern[rows, part_cols(h)], v)
+                row_sum[rows, :] = lanes if h == 0 else row_sum[rows, :] + lanes
+        h = n_part - 1
+        v = scale(prev, h)
+        acc = jnp.zeros((8, part_w), jnp.float32)
         for k in range(n_blk):
             rows = pl.ds(k * BLK, BLK)
-            u = p_col[rows, :] / jnp.sum(kern[rows, :] * v, axis=1, keepdims=True)
+            lanes = row_sum[rows, :] + row_lanes(kern[rows, part_cols(h)], v)
+            u = p_col[rows, :] / jnp.sum(lanes, axis=1, keepdims=True)
             u_ref[rows, :] = u
-            acc = acc + fold(kern[rows, :] * u)
-        total = group_sum(par, jnp.sum(acc, axis=0, keepdims=True))
-        return q_row[...] / total
+            acc = acc + fold(kern[rows, part_cols(0)] * u)
+        push(cur, 0, jnp.sum(acc, axis=0, keepdims=True))
+        for h in range(1, n_part):
+            push_part(cur, h)
+        return carry
 
     v_ref = loss_ref
 
     def outer(step, carry):
-        make_kernel(step)
-
-        def two_sweeps(i, v):
-            return sweep(1, sweep(0, v))
-
-        v_ref[...] = lax.fori_loop(0, SWEEPS // 2, two_sweeps, jnp.ones_like(q_row))
+        first_sweep(step)
+        lax.fori_loop(1, SWEEPS, sweep, 0)
+        for h in range(n_part):
+            v_ref[:, part_cols(h)] = scale((SWEEPS - 1) % 2, h)
         for c in range(n_chunk):
             cols = pl.ds(pl.multiple_of(me_c * width + c * LANES, LANES), LANES)
             for k in range(n_blk):
@@ -406,6 +457,8 @@
                 plan = u_ref[rows, :] * kern[rows, cols] * v_ref[:, cols]
                 t_ref[rows, c * LANES:(c + 1) * LANES] = plan
                 tp[me_r, c, rows, :] = plan.astype(jnp.bfloat16)
+            if c == 0:
+                t_start(0)
         cost((step + 1) % 2)
         return carry
 
@@ -418,8 +471,12 @@
         rows = pl.ds(k * BLK, BLK)
         block = (a_col[rows, :] + b_row[...]) - 2.0 * cross[rows, :]
         acc = acc + fold(block * (u_ref[rows, :] * kern[rows, :] * v))
-    total = group_sum(0, jnp.sum(acc, axis=0, keepdims=True))
-    loss_ref[...] = jnp.broadcast_to(jnp.sum(total, axis=1, keepdims=True), loss_ref.shape)
+    total = jnp.sum(acc, axis=0, keepdims=True)
+    half_sum = total[:, part_cols(0)]
+    for h in range(1, n_part):
+        half_sum = half_sum + total[:, part_cols(h)]
+    push(SWEEPS % 2, 0, half_sum)
+    loss_ref[...] = jnp.broadcast_to(jnp.sum(pull(SWEEPS % 2, 0), axis=1, keepdims=True), loss_ref.shape)
 
 
 def solution(mesh):
@@ -435,7 +492,7 @@
         vmem = pl.BlockSpec(memory_space=pltpu.VMEM)
         f32, b16, dma = jnp.float32, jnp.bfloat16, pltpu.SemaphoreType.DMA
         plan, loss = pl.pallas_call(
-            functools.partial(gw_kernel, n_rows, n_cols, n_steps),
+            functools.partial(gw_kernel, n_rows, n_cols, n_steps, N_PART),
             out_shape=(jax.ShapeDtypeStruct((height, width), f32), jax.ShapeDtypeStruct((1, full), f32)),
             in_specs=[pl.BlockSpec(memory_space=pltpu.SMEM), pl.BlockSpec(memory_space=pl.ANY)] + [vmem] * 4,
             out_specs=(vmem, vmem),
@@ -447,7 +504,8 @@
                 pltpu.VMEM((height, full), f32),
                 pltpu.VMEM((height, full), f32),
                 pltpu.VMEM((height, 1), f32),
-                pltpu.VMEM((2, n_rows, 1, full), f32),
+                pltpu.VMEM((height, LANES), f32),
+                pltpu.VMEM((2, N_PART, n_rows, 1, full // N_PART), f32),
                 pltpu.VMEM((2, height, PIECE), f32),
                 pltpu.VMEM((height, LANES), f32),
                 pltpu.VMEM((height, 1), f32),
@@ -463,7 +521,7 @@
                 pltpu.VMEM((n_cols, 1, height), f32),
                 dma((n_chunk, 14)), dma((n_rows, n_chunk, 2)),
                 dma((n_chunk, 6)), dma((2, n_cols, n_chunk, 2)),
-                dma((2, n_rows - 1)), dma((2, n_rows)),
+                dma((2, N_PART)), dma((2, N_PART)),
                 dma((3 * n_piece,)), dma((n_cols * n_piece,)),
                 dma((7, n_rows)), dma((7, n_rows)), dma((2,)),
             ],

time: 828 us -> 810 us (0.978)
  Pallas kernels: 823 us -> 806 us
    pallas_call x1, Pallas kernels: 823 us -> 806 us  [local_fn(): pl.pallas_call(functools.partial(gw_kernel, n_rows, n_cols, n_steps, N_PA...]
where the time goes in v3:
time: 810 us
  Pallas kernels  806 us (100%)
    pallas_call x1, Pallas kernels, local_fn(): pl.pallas_call(functools.partial(gw_kernel, n_rows, n_cols, n_steps, N_PA...  806 us

profile of v3, /device:TPU:97, one launch (start us, length us, event | category | flops | bytes accessed | tf_op | source)
XLA Modules:
  0.0 809.6 jit_solution(17272150645066826604)
XLA Ops:
  0.6 805.6 %shard_map.77 = (f32[1024,256]{1,0:T(8,128)}, f32[1,1024]{1,0:T(1,128)}) custom-call(f32[8]{0:T(128)} %eps_ref.1, f32[1024,2048]{1,0:T(8,128)} %c1_ref.1, f32[128,256]{1,0:T(8,128)} %c2_ref.1, f32[1024,256]{1,0:T(8,128)} %t0_ref.1, f32[1,1024]{1,0:T(1,128)} %bitcast.3, f32[1,256]{1,0:T(1,128)} %bitcast.4), custom_call_target="tpu_custom_call" | custom-call | tf_op jit(solution)/shard_map/pallas_call | solution.py:494
  806.3 1.1 slice.3
  807.4 2.3 copy.9

commit v4 on v3

--- a/solution.py
+++ b/solution.py
@@ -37,6 +37,8 @@
     right, left, far = row_id(1, core), row_id(-1, core), row_id(2, core)
     up, down, opp = (me_c + 1) % n_cols, (me_c + n_cols - 1) % n_cols, (me_c + 2) % n_cols
 
+    first_load = pltpu.make_async_copy(c1_ref.at[:, pl.ds(0, PIECE)], stage.at[0], ld_sem.at[0])
+    first_load.start()
     barrier = pltpu.get_barrier_semaphore()
     for d in range(1, n_rows):
         pl.semaphore_signal(barrier, inc=1, device_id={"rows": (me_r + d) % n_rows}, device_id_type=MESH)
@@ -64,17 +66,19 @@
 
     part_w = kern.shape[1] // n_part
 
-    def sum_copy(par, h, ref, d):
+    peers = [far, row_id(2, 1 - core), left, right, row_id(-1, 1 - core), row_id(1, 1 - core), sib]
+
+    def sum_copy(par, h, ref, target):
         return pltpu.make_async_remote_copy(src_ref=ref, dst_ref=ref, send_sem=s_send.at[par, h], recv_sem=s_recv.at[par, h],
-                                            device_id={"rows": (me_r + d) % n_rows}, device_id_type=MESH)
+                                            device_id={"rows": target}, device_id_type=MESH)
 
     def push(par, h, value):
         red[par, h, me_r] = value
-        for d in range(1, n_rows):
-            sum_copy(par, h, red.at[par, h, me_r], d).start()
+        for target in peers:
+            sum_copy(par, h, red.at[par, h, me_r], target).start()
 
     def pull(par, h):
-        every = sum_copy(par, h, red.at[par, h, pl.ds(0, n_rows - 1)], 1)
+        every = sum_copy(par, h, red.at[par, h, pl.ds(0, n_rows - 1)], sib)
         every.wait_recv()
         total = red[par, h, 0]
         for d in range(1, n_rows):
@@ -211,7 +215,6 @@
                                             recv_sem=c_recv.at[piece], device_id={"cols": target}, device_id_type=MESH)
 
     def prologue():
-        piece_load(0).start()
         p_all[me_r] = p_ref[...]
         p_fin = share(0, "rows", lambda s: p_all.at[s])
         q_all[me_c] = q_ref[...]
@@ -257,7 +260,7 @@
         sq = c2_ref[...] * c2_ref[...]
         b_red[me_r] = jnp.sum(sq * q_col[:, :1], axis=0, keepdims=True)
         b_fin = share(4, "rows", lambda s: b_red.at[s])
-        p_col[...] = jnp.broadcast_to(p_ref[...], (LANES, height)).T[:, :1]
+        p_col[...] = jnp.broadcast_to(p_ref[...], (LANES, height)).T
         c2y_fin()
         c2x_fin = share(5, "rows", lambda s: c2f.at[s])
         for k in range(n_chunk):
@@ -300,7 +303,7 @@
         total = a_red[0]
         for s in range(1, n_cols):
             total = total + a_red[s]
-        a_col[...] = jnp.broadcast_to(total, (LANES, height)).T[:, :1]
+        a_col[...] = jnp.broadcast_to(total, (LANES, height)).T
         ball_fin()
         b_row[...] = jnp.concatenate([b_all[k] for k in range(n_cols)], axis=1)
         c2x_fin()
@@ -391,30 +394,46 @@
     def part_cols(h):
         return slice(h * part_w, (h + 1) * part_w)
 
-    def row_lanes(block, weight):
-        total = None
-        for j in range(block.shape[1] // LANES):
-            cols = slice(j * LANES, (j + 1) * LANES)
-            term = block[:, cols] if weight is None else block[:, cols] * weight[:, cols]
-            total = term if total is None else total + term
+    def lane_tiles(ref, rows, cols):
+        return [ref[rows, j:j + LANES] for j in range(cols.start, cols.stop, LANES)]
+
+    def row_sums(tiles):
+        total = tiles[0]
+        for tile in tiles[1:]:
+            total = total + tile
         return total
+
+    def column_sums(tiles, u):
+        return jnp.concatenate([fold(tile * u) for tile in tiles], axis=1)
+
+    def row_scale(rows, lanes):
+        u = p_col[rows, :] / jnp.sum(lanes, axis=1, keepdims=True)
+        u_ref[rows, :] = u
+        return u
 
     def push_part(par, h):
         acc = jnp.zeros((8, part_w), jnp.float32)
         for k in range(n_blk):
             rows = pl.ds(k * BLK, BLK)
-            acc = acc + fold(kern[rows, part_cols(h)] * u_ref[rows, :])
+            acc = acc + column_sums(lane_tiles(kern, rows, part_cols(h)), u_ref[rows, :])
         push(par, h, jnp.sum(acc, axis=0, keepdims=True))
+
+    def cost_tiles(rows):
+        return [(a_col[rows, :] + b_row[:, j:j + LANES]) - 2.0 * cross[rows, j:j + LANES] for j in range(0, cross.shape[1], LANES)]
 
     def first_sweep(step):
         inv_eps = 1.0 / jnp.full((1, 1), eps_ref[step], jnp.float32)
         for k in range(n_blk):
             rows = pl.ds(k * BLK, BLK)
-            block = (a_col[rows, :] + b_row[...]) - 2.0 * cross[rows, :]
-            low = jnp.min(block, axis=1, keepdims=True)
-            block = jnp.exp((low - block) * inv_eps)
-            kern[rows, :] = block
-            u_ref[rows, :] = p_col[rows, :] / jnp.sum(row_lanes(block, None), axis=1, keepdims=True)
+            tiles = cost_tiles(rows)
+            low = tiles[0]
+            for tile in tiles[1:]:
+                low = jnp.minimum(low, tile)
+            low = jnp.min(low, axis=1, keepdims=True)
+            tiles = [jnp.exp((low - tile) * inv_eps) for tile in tiles]
+            for j, tile in enumerate(tiles):
+                kern[rows, j * LANES:(j + 1) * LANES] = tile
+            row_scale(rows, row_sums(tiles))
         for h in range(n_part):
             push_part(0, h)
 
@@ -423,21 +442,24 @@
 
     def sweep(i, carry):
         prev, cur = (i + 1) % 2, i % 2
+
+        def weighted(h, v):
+            def sums(rows):
+                tiles = lane_tiles(kern, rows, part_cols(h))
+                return row_sums([tile * v[:, j * LANES:(j + 1) * LANES] for j, tile in enumerate(tiles)])
+            return sums
+
         for h in range(n_part - 1):
-            v = scale(prev, h)
+            sums = weighted(h, scale(prev, h))
             for k in range(n_blk):
                 rows = pl.ds(k * BLK, BLK)
-                lanes = row_lanes(kern[rows, part_cols(h)], v)
-                row_sum[rows, :] = lanes if h == 0 else row_sum[rows, :] + lanes
-        h = n_part - 1
-        v = scale(prev, h)
+                row_sum[rows, :] = sums(rows) if h == 0 else row_sum[rows, :] + sums(rows)
+        sums = weighted(n_part - 1, scale(prev, n_part - 1))
         acc = jnp.zeros((8, part_w), jnp.float32)
         for k in range(n_blk):
             rows = pl.ds(k * BLK, BLK)
-            lanes = row_sum[rows, :] + row_lanes(kern[rows, part_cols(h)], v)
-            u = p_col[rows, :] / jnp.sum(lanes, axis=1, keepdims=True)
-            u_ref[rows, :] = u
-            acc = acc + fold(kern[rows, part_cols(0)] * u)
+            lanes = sums(rows) if n_part == 1 else row_sum[rows, :] + sums(rows)
+            acc = acc + column_sums(lane_tiles(kern, rows, part_cols(0)), row_scale(rows, lanes))
         push(cur, 0, jnp.sum(acc, axis=0, keepdims=True))
         for h in range(1, n_part):
             push_part(cur, h)
@@ -465,12 +487,11 @@
     prologue()
     lax.fori_loop(0, n_steps, outer, 0)
 
-    v = v_ref[...]
-    acc = jnp.zeros((8, v.shape[1]), jnp.float32)
+    acc = jnp.zeros((8, cross.shape[1]), jnp.float32)
     for k in range(n_blk):
         rows = pl.ds(k * BLK, BLK)
-        block = (a_col[rows, :] + b_row[...]) - 2.0 * cross[rows, :]
-        acc = acc + fold(block * (u_ref[rows, :] * kern[rows, :] * v))
+        plan = [u_ref[rows, :] * kern[rows, j:j + LANES] * v_ref[:, j:j + LANES] for j in range(0, cross.shape[1], LANES)]
+        acc = acc + jnp.concatenate([fold(x * y) for x, y in zip(cost_tiles(rows), plan)], axis=1)
     total = jnp.sum(acc, axis=0, keepdims=True)
     half_sum = total[:, part_cols(0)]
     for h in range(1, n_part):
@@ -503,13 +524,13 @@
                 pltpu.VMEM((n_chunk, height, LANES), f32),
                 pltpu.VMEM((height, full), f32),
                 pltpu.VMEM((height, full), f32),
-                pltpu.VMEM((height, 1), f32),
+                pltpu.VMEM((height, LANES), f32),
                 pltpu.VMEM((height, LANES), f32),
                 pltpu.VMEM((2, N_PART, n_rows, 1, full // N_PART), f32),
                 pltpu.VMEM((2, height, PIECE), f32),
                 pltpu.VMEM((height, LANES), f32),
-                pltpu.VMEM((height, 1), f32),
-                pltpu.VMEM((height, 1), f32),
+                pltpu.VMEM((height, LANES), f32),
+                pltpu.VMEM((height, LANES), f32),
                 pltpu.VMEM((1, full), f32),
                 pltpu.VMEM((1, full), f32),
                 pltpu.VMEM((n_rows, n_cols) + c2_blk.shape, b16),

time: 810 us -> 790 us (0.975)
  Pallas kernels: 806 us -> 785 us
    pallas_call x1, Pallas kernels: 806 us -> 785 us  [local_fn(): pl.pallas_call(functools.partial(gw_kernel, n_rows, n_cols, n_steps, N_PA...]
where the time goes in v4:
time: 790 us; the launch traced here: 789 us
  Pallas kernels  785 us (99%)
    pallas_call x1, Pallas kernels, local_fn(): pl.pallas_call(functools.partial(gw_kernel, n_rows, n_cols, n_steps, N_PA...  785 us

profile of v4, /device:TPU:97, one launch (start us, length us, event | category | flops | bytes accessed | tf_op | source)
XLA Modules:
  0.0 789.3 jit_solution(11558850120664194612)
XLA Ops:
  0.6 785.3 %shard_map.77 = (f32[1024,256]{1,0:T(8,128)}, f32[1,1024]{1,0:T(1,128)}) custom-call(f32[8]{0:T(128)} %eps_ref.1, f32[1024,2048]{1,0:T(8,128)} %c1_ref.1, f32[128,256]{1,0:T(8,128)} %c2_ref.1, f32[1024,256]{1,0:T(8,128)} %t0_ref.1, f32[1,1024]{1,0:T(1,128)} %bitcast.3, f32[1,256]{1,0:T(1,128)} %bitcast.4), custom_call_target="tpu_custom_call" | custom-call | tf_op jit(solution)/shard_map/pallas_call | solution.py:515
  786.0 1.1 slice.3
  787.1 2.3 copy.9

commit v5 on v4

--- a/solution.py
+++ b/solution.py
@@ -215,6 +215,25 @@
                                             recv_sem=c_recv.at[piece], device_id={"cols": target}, device_id_type=MESH)
 
     def prologue():
+        def piece_send(i):
+            piece = me_c * n_piece + i
+            c1s[piece] = stage[i % 2].astype(jnp.bfloat16)
+            piece_copy(piece, up, i).start()
+            piece_copy(piece, down, n_piece + i).start()
+
+        def piece_sum(i):
+            block = stage[i % 2]
+            where = (me_c * n_piece + i) * PIECE
+            p_row = p_all[where // height, :, pl.ds(pl.multiple_of(where % height, PIECE), PIECE)]
+            sq = block * block * p_row
+            acc = a_acc[...]
+            for k in range(PIECE // LANES):
+                acc = acc + sq[:, k * LANES:(k + 1) * LANES]
+            a_acc[...] = acc
+
+        piece_load(0).wait()
+        piece_load(1).start()
+        piece_send(0)
         p_all[me_r] = p_ref[...]
         p_fin = share(0, "rows", lambda s: p_all.at[s])
         q_all[me_c] = q_ref[...]
@@ -227,6 +246,7 @@
             t_start(k)
         a_acc[...] = jnp.zeros_like(a_acc)
         p_fin()
+        piece_sum(0)
 
         def own_piece(i, carry):
             piece_load(i).wait()
@@ -235,21 +255,11 @@
             def _():
                 piece_load(i + 1).start()
 
-            block = stage[i % 2]
-            piece = me_c * n_piece + i
-            c1s[piece] = block.astype(jnp.bfloat16)
-            piece_copy(piece, up, i).start()
-            piece_copy(piece, down, n_piece + i).start()
-            where = piece * PIECE
-            p_row = p_all[where // height, :, pl.ds(pl.multiple_of(where % height, PIECE), PIECE)]
-            sq = block * block * p_row
-            acc = a_acc[...]
-            for k in range(PIECE // LANES):
-                acc = acc + sq[:, k * LANES:(k + 1) * LANES]
-            a_acc[...] = acc
+            piece_send(i)
+            piece_sum(i)
             return carry
 
-        lax.fori_loop(0, n_piece, own_piece, 0)
+        lax.fori_loop(1, n_piece, own_piece, 0)
         q_fin()
         q_row[...] = jnp.concatenate([q_all[k] for k in range(n_cols)], axis=1)
         a_red[me_c] = jnp.sum(a_acc[...].T, axis=0, keepdims=True)
@@ -310,7 +320,7 @@
         depth = c2_ref.shape[0]
         for r in range(n_rows):
             for c in range(n_cols):
-                c2s[r * depth:(r + 1) * depth, c * width:(c + 1) * width] = c2f[r, c]
+                c2s[r * depth:(r + 1) * depth, c * width:(c + 1) * width] = c2f[r, c] * 2
         for i in range(n_piece):
             piece_copy(opp * n_piece + i, up, 0).wait_recv()
         group(opp)
@@ -333,7 +343,7 @@
         cross_add(0, whole(up))
         for k in range(n_chunk):
             a_far(0, k)
-        cross_add(0, whole(opp))
+        cross_add(0, [(opp, k) for k in range(n_chunk - 1)])
         a_done()
 
     def t_sib_part(chunk, chip_off, part):
@@ -384,7 +394,6 @@
         a_rest(par, 1)
         cross_add(par, [(down, 1), (up, 1)])
         a_far(par, 1)
-        cross_add(par, [(opp, 1)])
         t_done()
         a_done()
 
@@ -418,14 +427,17 @@
             acc = acc + column_sums(lane_tiles(kern, rows, part_cols(h)), u_ref[rows, :])
         push(par, h, jnp.sum(acc, axis=0, keepdims=True))
 
-    def cost_tiles(rows):
-        return [(a_col[rows, :] + b_row[:, j:j + LANES]) - 2.0 * cross[rows, j:j + LANES] for j in range(0, cross.shape[1], LANES)]
+    def cost_tiles(k, par):
+        rows = pl.ds(k * BLK, BLK)
+        last = pl.ds(pl.multiple_of(opp * width + (n_chunk - 1) * LANES, LANES), LANES)
+        twice = cross[rows, :] + jnp.dot(ap[par, opp, n_chunk - 1, rows, :], c2s[last, :], preferred_element_type=jnp.float32)
+        return [(a_col[rows, :] + b_row[:, j:j + LANES]) - twice[:, j:j + LANES] for j in range(0, cross.shape[1], LANES)]
 
     def first_sweep(step):
         inv_eps = 1.0 / jnp.full((1, 1), eps_ref[step], jnp.float32)
         for k in range(n_blk):
             rows = pl.ds(k * BLK, BLK)
-            tiles = cost_tiles(rows)
+            tiles = cost_tiles(k, step % 2)
             low = tiles[0]
             for tile in tiles[1:]:
                 low = jnp.minimum(low, tile)
@@ -491,7 +503,7 @@
     for k in range(n_blk):
         rows = pl.ds(k * BLK, BLK)
         plan = [u_ref[rows, :] * kern[rows, j:j + LANES] * v_ref[:, j:j + LANES] for j in range(0, cross.shape[1], LANES)]
-        acc = acc + jnp.concatenate([fold(x * y) for x, y in zip(cost_tiles(rows), plan)], axis=1)
+        acc = acc + jnp.concatenate([fold(x * y) for x, y in zip(cost_tiles(k, n_steps % 2), plan)], axis=1)
     total = jnp.sum(acc, axis=0, keepdims=True)
     half_sum = total[:, part_cols(0)]
     for h in range(1, n_part):

time: 790 us -> 787 us (level)
  no operation moved by 1% of the time
where the time goes in v5:
time: 787 us
  Pallas kernels  783 us (99%)
    pallas_call x1, Pallas kernels, local_fn(): pl.pallas_call(functools.partial(gw_kernel, n_rows, n_cols, n_steps, N_PA...  783 us

profile of v5, /device:TPU:97, one launch (start us, length us, event | category | flops | bytes accessed | tf_op | source)
XLA Modules:
  0.0 787.0 jit_solution(11581427061711493070)
XLA Ops:
  0.6 783.0 %shard_map.77 = (f32[1024,256]{1,0:T(8,128)}, f32[1,1024]{1,0:T(1,128)}) custom-call(f32[8]{0:T(128)} %eps_ref.1, f32[1024,2048]{1,0:T(8,128)} %c1_ref.1, f32[128,256]{1,0:T(8,128)} %c2_ref.1, f32[1024,256]{1,0:T(8,128)} %t0_ref.1, f32[1,1024]{1,0:T(1,128)} %bitcast.3, f32[1,256]{1,0:T(1,128)} %bitcast.4), custom_call_target="tpu_custom_call" | custom-call | tf_op jit(solution)/shard_map/pallas_call | solution.py:527
  783.7 1.1 slice.3
  784.8 2.3 copy.9
